TPU v7x, 32 devices: a whole 2x2x4 slice. The times are simulated.
32 devices in a mesh: gx: 2 (over y), gy: 4 (over x, core), gz: 4 (over z).
Axes of the slice: x: 2, y: 2, z: 4, core: 2. Of those that a mesh axis runs over, the one named last changes fastest.
Arguments:
- gradients: bfloat16 [32, 851968], P(('gx', 'gy', 'gz')), may hold values from -0.29882812 to 0.29882812
- master: float32 [851968], P(('gx', 'gy', 'gz')), may hold values from -6 to 6
- first_moment: float32 [851968], P(('gx', 'gy', 'gz')), may hold values from -3 to 3
- second_moment: float32 [851968], P(('gx', 'gy', 'gz')), may hold values from 0.01 to 1
- step_count: int32 [1], replicated, may hold values from 1 to 7
- step_size: float32 [1], replicated, may hold values from 0.01 to 0.1
Outputs:
- new_master: float32 [851968], P(('gx', 'gy', 'gz'))
- new_first: float32 [851968], P(('gx', 'gy', 'gz'))
- new_second: float32 [851968], P(('gx', 'gy', 'gz'))
- weights: bfloat16 [851968], replicated
All inputs are finite; a program needn't handle non-finite values.
Results may differ from a plain program's by a relative error of at most 0.009.
Values may be sent and summed in bfloat16 or wider, within the bound.
No kernel may reach another device: no remote copies, remote signals or barrier semaphores. Data moves between devices by JAX's collectives and lax.ppermute only.
A program may use at most 64 MiB of HBM per device.

v0:
```python
import jax
import jax.numpy as jnp
from jax import lax
from jax.sharding import PartitionSpec as P

BETA_ONE = 0.9
BETA_TWO = 0.95
EPSILON = 1e-08


def adam_update(summed, master, first_moment, second_moment, step_count, step_size):
    counted = step_count[0].astype(jnp.float32)
    first_fix = 1.0 - jnp.power(jnp.float32(BETA_ONE), counted)
    second_fix = 1.0 - jnp.power(jnp.float32(BETA_TWO), counted)
    new_first = BETA_ONE * first_moment + (1.0 - BETA_ONE) * summed
    new_second = BETA_TWO * second_moment + (1.0 - BETA_TWO) * summed * summed
    update = new_first / first_fix / (jnp.sqrt(new_second / second_fix) + EPSILON)
    new_master = master - step_size[0] * update
    return (new_master, new_first, new_second)


def per_device(gradients, master, first_moment, second_moment, step_count, step_size):
    count_x = lax.axis_size("gx")
    count_y = lax.axis_size("gy")
    count_z = lax.axis_size("gz")
    owned = master.shape[0]
    blocked = gradients.astype(jnp.float32).reshape(count_x * count_y, count_z, owned)
    blocked = lax.psum_scatter(
        blocked.astype(jnp.bfloat16), "gz", scatter_dimension=1, tiled=True
    ).astype(jnp.float32)
    blocked = lax.psum_scatter(
        blocked.astype(jnp.bfloat16), ("gx", "gy"), scatter_dimension=0, tiled=True
    ).astype(jnp.float32)
    summed = blocked.reshape(owned)
    new_master, new_first, new_second = adam_update(
        summed, master, first_moment, second_moment, step_count, step_size
    )
    rounded = new_master.astype(jnp.bfloat16)
    spread = rounded.reshape(1, 1, 1, owned)
    spread = lax.all_gather(spread, "gx", axis=0, tiled=True)
    spread = lax.all_gather(spread, "gy", axis=1, tiled=True)
    spread = lax.all_gather(spread, "gz", axis=2, tiled=True)
    weights = spread.reshape(count_x * count_y * count_z * owned)
    return (new_master, new_first, new_second, weights)


def solution(mesh):
    in_specs = (
        P(("gx", "gy", "gz"), None),
        P(("gx", "gy", "gz")),
        P(("gx", "gy", "gz")),
        P(("gx", "gy", "gz")),
        P(),
        P(),
    )
    out_specs = (P(("gx", "gy", "gz")), P(("gx", "gy", "gz")), P(("gx", "gy", "gz")), P())
    return jax.shard_map(
        per_device, mesh=mesh, in_specs=in_specs, out_specs=out_specs, check_vma=False
    )
```

profile of v0, /device:TPU:0, one launch (start us, length us, event | category | flops | bytes accessed | tf_op | source)
XLA Modules:
  0.0 208.7 jit_solution(14987365849676348924)
XLA Ops:
  7.2 0.0 reduce-scatter.2.cloned.1.call-start
  7.2 36.4 %reduce = bf16[851968]{0:T(1024)(128)(2,1)S(1)} reduce(bf16[1,851968]{1,0:T(2,128)(2,1)} %param.6, bf16[]{:T(256)} %constant.25), dimensions={0}, to_apply=%param.6.reduce_sub_computation | reduce | bytes 3407874 | tf_op args[0]
  43.6 0.6 convert_element_type.15
  44.2 2.1 %copy.13 = bf16[8,4,26624]{2,0,1:T(8,128)(2,1)} copy(bf16[8,4,26624]{2,1,0:T(4,128)(2,1)S(1)} %convert_element_type.15) | data formatting | bytes 3407872 | tf_op jit(solution)/shard_map/convert_element_type | solution.py:29
  46.4 0.0 reduce-scatter.2.cloned.1.call-update
  46.4 0.0 all-reduce.3.cloned.1.call-start
  46.4 40.3 %reduce-scatter.2.cloned.1.call-done = bf16[8,1,26624]{2,0,1:T(8,128)(2,1)} async-done(((bf16[8,4,26624]{2,0,1:T(8,128)(2,1)}), bf16[8,1,26624]{2,0,1:T(8,128)(2,1)}) %reduce-scatter.2.cloned.1.call-update) | async-done | bytes 426000 | tf_op jit(solution)/shard_map/reduce_scatter | solution.py:28
  86.7 2.6 %copy.14 = bf16[8,1,26624]{2,1,0:T(2,128)(2,1)} copy(bf16[8,1,26624]{2,0,1:T(8,128)(2,1)} %reduce-scatter.2.cloned.1.call-done) | data formatting | bytes 851968 | tf_op jit(solution)/shard_map/reduce_scatter | solution.py:28
  89.3 0.0 all-reduce.3.cloned.1.call-update
  89.3 0.0 all-gather.3.cloned.1.call-start
  90.7 0.0 copy-done.3
  90.7 0.6 dynamic-slice
  91.3 54.0 %all-reduce.3.cloned.1.call-done = bf16[8,1,26624]{2,1,0:T(2,128)(2,1)} async-done(((bf16[8,1,26624]{2,1,0:T(2,128)(2,1)}), bf16[8,1,26624]{2,1,0:T(2,128)(2,1)}) %all-reduce.3.cloned.1.call-update) | async-done | bytes 426000
  145.4 1.7 dynamic-slice_convert_fusion
  147.0 0.0 copy-done
  147.0 0.0 copy-done.1
  147.0 0.0 copy-done.2
  147.0 0.8 fusion.1
  147.8 4.8 %all-gather = bf16[53248]{0:T(1024)(128)(2,1)S(1)} all-gather(bf16[26624]{0:T(1024)(128)(2,1)S(1)} %get-tuple-element.4), channel_id=2, replica_groups=mesh['gx'=2,'gy'=4,'gz'=4] {'gx'}, dimensions={0}, use_global_device_ids=true | all-gather | bytes 159744 | tf_op jit(solution)/shard_map/all_gather | solution.py:40
  152.6 6.7 %all_gather.10 = bf16[2,4,1,26624]{3,0,2,1:T(2,128)(2,1)} all-gather(bf16[2,1,1,26624]{3,0,2,1:T(2,128)(2,1)S(1)} %reshape.37), channel_id=1, replica_groups=mesh['gx'=2,'gy'=4,'gz'=4] {'gy'}, dimensions={1}, use_global_device_ids=true | all-gather | bytes 532480 | tf_op jit(solution)/shard_map/all_gather | solution.py:41
  159.3 0.0 all-gather.3.cloned.1.call-update
  159.3 39.0 %all-gather.3.cloned.1.call-done = bf16[2,4,4,26624]{3,0,2,1:T(2,128)(2,1)} async-done(((bf16[2,4,1,26624]{3,0,2,1:T(2,128)(2,1)}), bf16[2,4,4,26624]{3,0,2,1:T(2,128)(2,1)}) %all-gather.3.cloned.1.call-update) | async-done | bytes 1703952 | tf_op jit(solution)/shard_map/all_gather | solution.py:42
  198.3 2.3 %copy.15 = bf16[2,4,4,26624]{3,2,1,0:T(4,128)(2,1)S(1)} copy(bf16[2,4,4,26624]{3,0,2,1:T(2,128)(2,1)} %all-gather.3.cloned.1.call-done) | data formatting | bytes 3407872 | tf_op jit(solution)/shard_map/all_gather | solution.py:42
  200.7 1.5 copy.16
  (5 shorter events, 0.0 us)
Async XLA Ops:
  7.2 79.6 %reduce-scatter.2.cloned.1.call-start = ((), (), s32[]{:S(2)}) async-start(), calls=%async_computation.1 | async-start | bytes 2129920 | tf_op jit(solution)/shard_map/reduce_scatter | solution.py:28
  46.3 44.4 %copy-start.3 = (u32[32]{0:T(128)S(1)}, u32[32]{0:T(128)}, u32[]{:S(2)}) copy-start(u32[32]{0:T(128)} %constant.23) | copy-start | bytes 388
  46.3 100.7 %copy-start = (f32[26624]{0:T(1024)S(1)}, f32[26624]{0:T(1024)}, u32[]{:S(2)}) copy-start(f32[26624]{0:T(1024)} %param.7) | copy-start | bytes 319492
  46.3 100.7 %copy-start.1 = (f32[26624]{0:T(1024)S(1)}, f32[26624]{0:T(1024)}, u32[]{:S(2)}) copy-start(f32[26624]{0:T(1024)} %param.9) | copy-start | bytes 319492
  46.4 100.7 %copy-start.2 = (f32[26624]{0:T(1024)S(1)}, f32[26624]{0:T(1024)}, u32[]{:S(2)}) copy-start(f32[26624]{0:T(1024)} %param.8) | copy-start | bytes 319492
  46.4 99.0 %all-reduce.3.cloned.1.call-start = ((), (), s32[]{:S(2)}) async-start(), calls=%async_computation.3 | async-start | bytes 1703936
  89.3 109.0 %all-gather.3.cloned.1.call-start = ((), (), s32[]{:S(2)}) async-start(), calls=%async_computation.2 | async-start | bytes 2129920 | tf_op jit(solution)/shard_map/all_gather | solution.py:42
Sparse Core Ops, SparseCore 0:
  46.5 40.1 reduce-scatter.1
  90.5 54.8 all-reduce.2
  159.5 38.8 all-gather.2
where the time goes:
time: 209 us
  waiting for transfers between devices  133 us (64%)
  other arithmetic  38.8 us (19%)
  between operations  15.2 us (7%)
  blocking collectives  11.5 us (6%)
  local copies, waits for them, and re-layouts  9.69 us (5%)
    unnamed x4, waiting for transfers between devices  54.1 us
    reduce_scatter x1, waiting for transfers between devices, per_device(): lax.psum_scatter(blocked.astype(jnp.bfloat16), 'gz', scatter_dimension=1,...  40.3 us
    all_gather x1, waiting for transfers between devices, per_device(): spread = lax.all_gather(spread, 'gz', axis=2, tiled=True)  39 us
    unnamed x1, other arithmetic  36.4 us
    all_gather x1, blocking collectives, per_device(): spread = lax.all_gather(spread, 'gy', axis=1, tiled=True)  6.68 us
    all_gather x1, blocking collectives, per_device(): spread = lax.all_gather(spread, 'gx', axis=0, tiled=True)  4.79 us
  transfers between devices with their start and end apart: 3, of which 3 were waited for; matrix products, arithmetic and copies ran while one was open for 0% of the time, Pallas kernels for 0%

commit v1 on v0

v1 whole, which is shorter than its diff:
```python
import itertools

import jax
import jax.numpy as jnp
from jax import lax
from jax.experimental import pallas as pl
from jax.experimental.pallas import tpu as pltpu
from jax.sharding import PartitionSpec as P


BETA_ONE = 0.9
BETA_TWO = 0.95
EPSILON = 1e-08
LANES = 128
VMEM_LIMIT = 8 << 20
FIRST = 2
X, PAIR, HIGH, LOW = range(4)
SUM_STAGES = ((X, PAIR, LOW), (HIGH,))
SPREAD_STAGES = ((HIGH, LOW), (X, PAIR))


def adam_update(summed, master, first_moment, second_moment, step_count, step_size):
    counted = step_count[0].astype(jnp.float32)
    first_fix = 1.0 - jnp.power(jnp.float32(BETA_ONE), counted)
    second_fix = 1.0 - jnp.power(jnp.float32(BETA_TWO), counted)
    new_first = BETA_ONE * first_moment + (1.0 - BETA_ONE) * summed
    new_second = BETA_TWO * second_moment + (1.0 - BETA_TWO) * summed * summed
    update = new_first / first_fix / (jnp.sqrt(new_second / second_fix) + EPSILON)
    new_master = master - step_size[0] * update
    return (new_master, new_first, new_second)


class Places:
    def __init__(self):
        self.x, self.y, self.z = (lax.axis_size(a) for a in ("gx", "gy", "gz"))
        self.sizes = (self.x, self.y // 2, self.z // 2, 2)

    def offsets(self, digits):
        every = itertools.product(*(range(n if i in digits else 1) for i, n in enumerate(self.sizes)))
        return sorted(every, key=lambda o: (not any(o), sum(v > 0 for v in o)))

    def block(self, sign, offset, other):
        at_x, at_y, at_z = (lax.axis_index(a) for a in ("gx", "gy", "gz"))
        place = (at_x, lax.div(at_y, 2), lax.div(at_z, 2), lax.rem(at_z, 2))
        x, pair, high, low = (
            lax.rem(at + n + sign * o, n) if o else at for at, n, o in zip(place, self.sizes, offset)
        )
        side = lax.rem(at_y, 2)
        side = 1 - side if other else side
        return ((x * self.sizes[1] + pair) * 2 + side) * self.z + high * 2 + low

    def send(self, value, offset):
        moves = []
        for x, pair, side, high, low in itertools.product(
            *(range(n) for n in (*self.sizes[:2], 2, *self.sizes[2:]))
        ):
            to = [(v + o) % n for v, o, n in zip((x, pair, high, low), offset, self.sizes)]
            source, target = (
                ((p[0] * self.sizes[1] + p[1]) * 2 + side) * self.z + p[2] * 2 + p[3]
                for p in ((x, pair, high, low), to)
            )
            moves.append((source, target))
        return lax.ppermute(value, ("gx", "gy", "gz"), moves)

    def swap(self, value):
        return lax.ppermute(value, "gy", [(y, y ^ 1) for y in range(self.y)])


def both(one, two):
    return tuple(a + b for a, b in zip(one, two))


def dense_blocks(gradients, offsets, block, places, after):
    rows = block // LANES
    total = len(offsets) * rows

    def kernel(g_ref, *refs):
        keep_ref, send_ref = refs[len(after) :]
        for other, out_ref in ((True, send_ref), (False, keep_ref)):
            for slot, offset in enumerate(offsets):
                start = pl.multiple_of(places.block(1, offset, other) * block, LANES)
                out_ref[slot * rows : (slot + 1) * rows, :] = g_ref[0, pl.ds(start, block)].reshape(rows, LANES)

    out = jax.ShapeDtypeStruct((total, LANES), gradients.dtype)
    return pl.pallas_call(
        kernel,
        in_specs=[pl.BlockSpec(memory_space=pltpu.VMEM)] + [pl.BlockSpec(memory_space=pl.ANY)] * len(after),
        out_specs=[pl.BlockSpec(memory_space=pltpu.VMEM)] * 2,
        out_shape=[out, out],
        compiler_params=pltpu.CompilerParams(vmem_limit_bytes=VMEM_LIMIT),
        cost_estimate=pl.CostEstimate(
            flops=8 * total * LANES, bytes_accessed=12 * total * LANES, transcendentals=0
        ),
    )(gradients, *after)


def place_blocks(pieces, held, block, total, places):
    rows = block // LANES
    if rows % 8:
        where = jnp.stack([places.block(-1, *one) for one in held])
        found = jnp.concatenate(pieces).reshape(-1, block)
        return jnp.zeros_like(found).at[where].set(found).reshape(-1, LANES)

    def kernel(*refs):
        sources, out_ref, sems = refs[: len(pieces)], refs[len(pieces)], refs[len(pieces) + 1]
        copies = []
        for source in sources:
            for k in range(source.shape[0] // rows):
                at = len(copies)
                start = pl.multiple_of(places.block(-1, *held[at]) * rows, 8)
                copies.append(
                    pltpu.make_async_copy(
                        source.at[pl.ds(k * rows, rows)], out_ref.at[pl.ds(start, rows)], sems.at[at]
                    )
                )
        for copy in copies:
            copy.start()
        for copy in copies:
            copy.wait()

    return pl.pallas_call(
        kernel,
        in_specs=[pl.BlockSpec(memory_space=pl.ANY)] * len(pieces),
        out_specs=pl.BlockSpec(memory_space=pl.ANY),
        out_shape=jax.ShapeDtypeStruct((total // LANES, LANES), pieces[0].dtype),
        scratch_shapes=[pltpu.SemaphoreType.DMA((len(held),))],
        compiler_params=pltpu.CompilerParams(vmem_limit_bytes=VMEM_LIMIT),
        cost_estimate=pl.CostEstimate(flops=total, bytes_accessed=4 * total, transcendentals=0),
    )(*pieces)


def per_device(gradients, master, first_moment, second_moment, step_count, step_size):
    places = Places()
    owned = master.shape[0]
    rows = owned // LANES
    wide, narrow = jnp.float32, gradients.dtype

    near, far = (places.offsets(digits) for digits in SUM_STAGES)
    size = len(far) * rows
    arrived, after = [], []
    for part in (near[:FIRST], near[FIRST:]):
        keep, send = dense_blocks(gradients, [both(o, f) for o in part for f in far], owned, places, after)
        after = [send]
        got = places.swap(send)
        for slot, offset in enumerate(part):
            span = slice(slot * size, (slot + 1) * size)
            value = keep[span].astype(wide) + got[span].astype(wide)
            if any(offset):
                arrived.append(places.send(value.astype(narrow), offset))
            else:
                total = value
    for part in arrived:
        total = total + part.astype(wide)
    moved = []
    for slot, offset in enumerate(far[:-1]):
        moved.append(places.send(total[slot * rows : (slot + 1) * rows].astype(narrow), offset))
    summed = total[-rows:]
    for part in moved:
        summed = summed + part.astype(wide)

    new_master, new_first, new_second = adam_update(
        summed.reshape(owned), master, first_moment, second_moment, step_count, step_size
    )

    far, near = (places.offsets(digits) for digits in SPREAD_STAGES)
    line = [new_master.astype(narrow).reshape(rows, LANES)] * len(far)
    for slot, offset in enumerate(far[:-1]):
        line[slot] = places.send(line[-1], offset)
    line = jnp.concatenate(line, axis=0)
    pieces = [line] * len(near)
    for slot, offset in enumerate(near[:-1]):
        pieces[slot] = places.send(line, offset)
    pieces = pieces + [places.swap(piece) for piece in pieces]
    held = [(both(o, f), other) for other in (False, True) for o in near for f in far]
    weights = place_blocks(pieces, held, owned, gradients.shape[1], places)
    return (new_master, new_first, new_second, weights.reshape(-1))


def solution(mesh):
    in_specs = (
        P(("gx", "gy", "gz"), None),
        P(("gx", "gy", "gz")),
        P(("gx", "gy", "gz")),
        P(("gx", "gy", "gz")),
        P(),
        P(),
    )
    out_specs = (P(("gx", "gy", "gz")), P(("gx", "gy", "gz")), P(("gx", "gy", "gz")), P())

    return jax.shard_map(per_device, mesh=mesh, in_specs=in_specs, out_specs=out_specs, check_vma=False)
```

time: 209 us -> 48.6 us (0.23)
  waiting for transfers between devices: 133 us -> 19.3 us
  other arithmetic: 38.8 us -> 1.12 us
  starting transfers between devices: 0.12 us -> 22.2 us
  between operations: 15.2 us -> 2.11 us
  blocking collectives: 11.5 us -> 0 us
  local copies, waits for them, and re-layouts: 9.69 us -> 1.98 us
    unnamed x4 -> x0, waiting for transfers between devices: 54.1 us -> none
    reduce_scatter x1 -> x0, waiting for transfers between devices: 40.3 us -> none  [per_device(): lax.psum_scatter(blocked.astype(jnp.bfloat16), 'gz', scatter_dimension=1,...]
    all_gather x1 -> x0, waiting for transfers between devices: 39 us -> none  [per_device(): spread = lax.all_gather(spread, 'gz', axis=2, tiled=True)]
    unnamed x1 -> x0, other arithmetic: 36.4 us -> none
    ppermute x0 -> x20, starting transfers between devices: none -> 22.2 us  [the longest x14 21.1 us: send(): return lax.ppermute(value, ('gx', 'gy', 'gz'), moves)]
    ppermute x0 -> x20, waiting for transfers between devices: none -> 19.3 us  [the longest x14 16.1 us: send(): return lax.ppermute(value, ('gx', 'gy', 'gz'), moves)]
    all_gather x2 -> x0, blocking collectives: 11.5 us -> none  [the longest x1 6.68 us: per_device(): spread = lax.all_gather(spread, 'gy', axis=1, tiled=True)]
    convert_element_type x2 -> x0, local copies, waits for them, and re-layouts: 2.71 us -> none  [per_device(): blocked.astype(jnp.bfloat16)]
  transfers between devices with their start and end apart: 3 -> 20, of which waited for: 3 -> 10; matrix products, arithmetic and copies ran while one was open for 0% -> 0% of each run, Pallas kernels for 0% -> 0%
where the time goes in v1:
time: 48.6 us; the launch traced here: 48.4 us
  starting transfers between devices  22.2 us (46%)
  waiting for transfers between devices  19.3 us (40%)
  between operations  2.11 us (4%)
  local copies, waits for them, and re-layouts  1.98 us (4%)
  Pallas kernels  1.7 us (3%)
  other arithmetic  1.12 us (2%)
    ppermute x14, starting transfers between devices, send(): return lax.ppermute(value, ('gx', 'gy', 'gz'), moves)  21.1 us
    ppermute x14, waiting for transfers between devices, send(): return lax.ppermute(value, ('gx', 'gy', 'gz'), moves)  16.1 us
    ppermute x6, waiting for transfers between devices, swap(): return lax.ppermute(value, 'gy', [(y, y ^ 1) for y in range(self.y)])  3.18 us
    unnamed x8, local copies, waits for them, and re-layouts  1.98 us
    pallas_call x1, Pallas kernels, place_blocks(): pl.pallas_call(kernel, in_specs=[pl.BlockSpec(memory_space=pl.ANY)] * len...  1.44 us
    ppermute x6, starting transfers between devices, swap(): return lax.ppermute(value, 'gy', [(y, y ^ 1) for y in range(self.y)])  1.1 us
  transfers between devices with their start and end apart: 20, of which 10 were waited for; matrix products, arithmetic and copies ran while one was open for 0% of the time, Pallas kernels for 0%

profile of v1, /device:TPU:0, one launch (start us, length us, event | category | flops | bytes accessed | tf_op | source)
XLA Modules:
  0.0 48.4 jit_solution(6200521097832253212)
XLA Ops:
  0.6 2.0 %copy-done = bf16[1,851968]{1,0:T(2,128)(2,1)S(1)} copy-done((bf16[1,851968]{1,0:T(2,128)(2,1)S(1)}, bf16[1,851968]{1,0:T(2,128)(2,1)}, u32[]{:S(2)}) %copy-start) | copy-done | bytes 1703960
  2.9 0.6 %collective-permute-start = (bf16[2496,128]{1,0:T(8,128)(2,1)S(1)}, bf16[2496,128]{1,0:T(8,128)(2,1)S(1)}, u32[]{:S(2)}, u32[]{:S(2)}) collective-permute-start(bf16[2496,128]{1,0:T(8,128)(2,1)S(1)} %get-tuple-element.10), channel_id=1, source_target_pairs={{0,4},{4,0},{8,12},{12,8},{1,5},{5,1},{9,13},{13,9},{2,6},{6,2},{1... | collective-permute-start | bytes 1916936 | tf_op jit(solution)/shard_map/ppermute | solution.py:66
  3.5 1.9 %collective-permute-done.1 = bf16[832,128]{1,0:T(8,128)(2,1)S(1)} collective-permute-done((bf16[832,128]{1,0:T(8,128)(2,1)S(1)}, bf16[832,128]{1,0:T(8,128)(2,1)S(1)}, u32[]{:S(2)}, u32[]{:S(2)}) %collective-permute-start.1) | collective-permute-done | bytes 213024 | tf_op jit(solution)/shard_map/ppermute | solution.py:66
  5.5 3.0 %collective-permute-start.2 = (bf16[416,128]{1,0:T(8,128)(2,1)S(1)}, bf16[416,128]{1,0:T(8,128)(2,1)S(1)}, u32[]{:S(2)}, u32[]{:S(2)}) collective-permute-start(bf16[416,128]{1,0:T(8,128)(2,1)S(1)} %get-tuple-element.21), channel_id=1, source_target_pairs={{0,1},{1,0},{2,3},{3,2},{4,5},{5,4},{6,7},{7,6},{8,9},{9,8},{10,11... | collective-permute-start | bytes 319496 | tf_op jit(solution)/shard_map/ppermute | solution.py:63
  8.5 1.5 %collective-permute-start.3 = (bf16[416,128]{1,0:T(8,128)(2,1)S(1)}, bf16[416,128]{1,0:T(8,128)(2,1)S(1)}, u32[]{:S(2)}, u32[]{:S(2)}) collective-permute-start(bf16[416,128]{1,0:T(8,128)(2,1)S(1)} %get-tuple-element.22), channel_id=1, source_target_pairs={{0,8},{1,9},{2,10},{3,11},{4,12},{5,13},{6,14},{7,15},{8,0},{9,1},... | collective-permute-start | bytes 319496 | tf_op jit(solution)/shard_map/ppermute | solution.py:63
  10.2 1.6 %collective-permute-start.4 = (bf16[416,128]{1,0:T(8,128)(2,1)S(1)}, bf16[416,128]{1,0:T(8,128)(2,1)S(1)}, u32[]{:S(2)}, u32[]{:S(2)}) collective-permute-start(bf16[416,128]{1,0:T(8,128)(2,1)S(1)} %get-tuple-element.16), channel_id=1, source_target_pairs={{0,16},{1,17},{2,18},{3,19},{4,20},{5,21},{6,22},{7,23},{8,24},{9,... | collective-permute-start | bytes 319496 | tf_op jit(solution)/shard_map/ppermute | solution.py:63
  11.8 2.8 %collective-permute-start.7 = (bf16[416,128]{1,0:T(8,128)(2,1)S(1)}, bf16[416,128]{1,0:T(8,128)(2,1)S(1)}, u32[]{:S(2)}, u32[]{:S(2)}) collective-permute-start(bf16[416,128]{1,0:T(8,128)(2,1)S(1)} %get-tuple-element.18), channel_id=1, source_target_pairs={{0,24},{1,25},{2,26},{3,27},{4,28},{5,29},{6,30},{7,31},{8,16},{9,... | collective-permute-start | bytes 319496 | tf_op jit(solution)/shard_map/ppermute | solution.py:63
  14.6 1.5 %collective-permute-start.6 = (bf16[416,128]{1,0:T(8,128)(2,1)S(1)}, bf16[416,128]{1,0:T(8,128)(2,1)S(1)}, u32[]{:S(2)}, u32[]{:S(2)}) collective-permute-start(bf16[416,128]{1,0:T(8,128)(2,1)S(1)} %get-tuple-element.19), channel_id=1, source_target_pairs={{0,17},{1,16},{2,19},{3,18},{4,21},{5,20},{6,23},{7,22},{8,25},{9,... | collective-permute-start | bytes 319496 | tf_op jit(solution)/shard_map/ppermute | solution.py:63
  16.2 5.6 %collective-permute-done.4 = bf16[416,128]{1,0:T(8,128)(2,1)S(1)} collective-permute-done((bf16[416,128]{1,0:T(8,128)(2,1)S(1)}, bf16[416,128]{1,0:T(8,128)(2,1)S(1)}, u32[]{:S(2)}, u32[]{:S(2)}) %collective-permute-start.4) | collective-permute-done | bytes 106528 | tf_op jit(solution)/shard_map/ppermute | solution.py:63
  22.0 2.7 %collective-permute-start.9 = (bf16[208,128]{1,0:T(8,128)(2,1)S(1)}, bf16[208,128]{1,0:T(8,128)(2,1)S(1)}, u32[]{:S(2)}, u32[]{:S(2)}) collective-permute-start(bf16[208,128]{1,0:T(8,128)(2,1)S(1)} %slice.107), channel_id=1, source_target_pairs={{0,2},{1,3},{2,0},{3,1},{4,6},{5,7},{6,4},{7,5},{8,10},{9,11},{10,... | collective-permute-start | bytes 159752 | tf_op jit(solution)/shard_map/ppermute | solution.py:63
  26.0 1.6 %collective-permute-done.9 = bf16[208,128]{1,0:T(8,128)(2,1)S(1)} collective-permute-done((bf16[208,128]{1,0:T(8,128)(2,1)S(1)}, bf16[208,128]{1,0:T(8,128)(2,1)S(1)}, u32[]{:S(2)}, u32[]{:S(2)}) %collective-permute-start.9) | collective-permute-done | bytes 53280 | tf_op jit(solution)/shard_map/ppermute | solution.py:63
  27.6 0.8 %convert_bitcast_fusion = (bf16[208,128]{1,0:T(8,128)(2,1)S(1)}, f32[26624]{0:T(1024)}, f32[26624]{0:T(1024)}, f32[26624]{0:T(1024)}) fusion(f32[26624]{0:T(1024)S(1)} %copy-done.1, f32[]{:T(128)} %bitcast.3, f32[]{:T(128)} %bitcast.2, f32[]{:T(128)} %bitcast.14, bf16[208,128]{1,0:T(8,128)(2,1)S(1)} %collective-permute-done.9, ...), kind=kLoop, calls=%fused_computation.16 | loop fusion | flops 425984 | bytes 851980 | tf_op jit(solution)/shard_map/reshape | solution.py:166
  28.4 2.4 %collective-permute-start.12 = (bf16[208,128]{1,0:T(8,128)(2,1)S(1)}, bf16[208,128]{1,0:T(8,128)(2,1)S(1)}, u32[]{:S(2)}, u32[]{:S(2)}) collective-permute-start(bf16[208,128]{1,0:T(8,128)(2,1)S(1)} %get-tuple-element.12), channel_id=1, source_target_pairs={{0,3},{1,2},{2,1},{3,0},{4,7},{5,6},{6,5},{7,4},{8,11},{9,10},{10,... | collective-permute-start | bytes 159752 | tf_op jit(solution)/shard_map/ppermute | solution.py:63
  30.8 2.0 %collective-permute-start.10 = (bf16[208,128]{1,0:T(8,128)(2,1)S(1)}, bf16[208,128]{1,0:T(8,128)(2,1)S(1)}, u32[]{:S(2)}, u32[]{:S(2)}) collective-permute-start(bf16[208,128]{1,0:T(8,128)(2,1)S(1)} %get-tuple-element.12), channel_id=1, source_target_pairs={{0,1},{1,0},{2,3},{3,2},{4,5},{5,4},{6,7},{7,6},{8,9},{9,8},{10,11... | collective-permute-start | bytes 159752 | tf_op jit(solution)/shard_map/ppermute | solution.py:63
  32.8 1.5 %collective-permute-done.12 = bf16[208,128]{1,0:T(8,128)(2,1)S(1)} collective-permute-done((bf16[208,128]{1,0:T(8,128)(2,1)S(1)}, bf16[208,128]{1,0:T(8,128)(2,1)S(1)}, u32[]{:S(2)}, u32[]{:S(2)}) %collective-permute-start.12) | collective-permute-done | bytes 53280 | tf_op jit(solution)/shard_map/ppermute | solution.py:63
  34.3 1.7 %collective-permute-done.11 = bf16[208,128]{1,0:T(8,128)(2,1)S(1)} collective-permute-done((bf16[208,128]{1,0:T(8,128)(2,1)S(1)}, bf16[208,128]{1,0:T(8,128)(2,1)S(1)}, u32[]{:S(2)}, u32[]{:S(2)}) %collective-permute-start.11) | collective-permute-done | bytes 53280 | tf_op jit(solution)/shard_map/ppermute | solution.py:63
  36.1 2.3 %collective-permute-start.15 = (bf16[832,128]{1,0:T(8,128)(2,1)S(1)}, bf16[832,128]{1,0:T(8,128)(2,1)S(1)}, u32[]{:S(2)}, u32[]{:S(2)}) collective-permute-start(bf16[832,128]{1,0:T(8,128)(2,1)S(1)} %pad_maximum_fusion.refs_3_), channel_id=1, source_target_pairs={{0,24},{1,25},{2,26},{3,27},{4,28},{5,29},{6,30},{7,31},{8,16},{9,... | collective-permute-start | bytes 638984 | tf_op jit(solution)/shard_map/ppermute | solution.py:63
  38.6 1.0 %collective-permute-start.13 = (bf16[832,128]{1,0:T(8,128)(2,1)S(1)}, bf16[832,128]{1,0:T(8,128)(2,1)S(1)}, u32[]{:S(2)}, u32[]{:S(2)}) collective-permute-start(bf16[832,128]{1,0:T(8,128)(2,1)S(1)} %pad_maximum_fusion.refs_3_), channel_id=1, source_target_pairs={{0,8},{1,9},{2,10},{3,11},{4,12},{5,13},{6,14},{7,15},{8,0},{9,1},... | collective-permute-start | bytes 638984 | tf_op jit(solution)/shard_map/ppermute | solution.py:63
  39.6 3.4 %collective-permute-done.15.refs_2_ = bf16[832,128]{1,0:T(8,128)(2,1)S(1)} collective-permute-done((bf16[832,128]{1,0:T(8,128)(2,1)S(1)}, bf16[832,128]{1,0:T(8,128)(2,1)S(1)}, u32[]{:S(2)}, u32[]{:S(2)}) %collective-permute-start.15) | collective-permute-done | bytes 213024 | tf_op jit(solution)/shard_map/ppermute | solution.py:63
  43.0 2.2 %collective-permute-done.14.refs_1_ = bf16[832,128]{1,0:T(8,128)(2,1)S(1)} collective-permute-done((bf16[832,128]{1,0:T(8,128)(2,1)S(1)}, bf16[832,128]{1,0:T(8,128)(2,1)S(1)}, u32[]{:S(2)}, u32[]{:S(2)}) %collective-permute-start.14) | collective-permute-done | bytes 213024 | tf_op jit(solution)/shard_map/ppermute | solution.py:63
  45.2 0.5 collective-permute-start.16
  45.7 0.9 %collective-permute-done.17.refs_5_ = bf16[832,128]{1,0:T(8,128)(2,1)S(1)} collective-permute-done((bf16[832,128]{1,0:T(8,128)(2,1)S(1)}, bf16[832,128]{1,0:T(8,128)(2,1)S(1)}, u32[]{:S(2)}, u32[]{:S(2)}) %collective-permute-start.17) | collective-permute-done | bytes 213024 | tf_op jit(solution)/shard_map/ppermute | solution.py:66
  46.6 0.3 collective-permute-done.16.refs_4_
  47.0 1.4 %shard_map.95 = bf16[6656,128]{1,0:T(8,128)(2,1)} custom-call(bf16[832,128]{1,0:T(8,128)(2,1)S(1)} %collective-permute-done.13.refs_0_, bf16[832,128]{1,0:T(8,128)(2,1)S(1)} %collective-permute-done.14.refs_1_, bf16[832,128]{1,0:T(8,128)(2,1)S(1)} %collective-permute-done.15.refs_2_, bf16[832,128]{1,0:T(8,128)(2,1)S(1)} %pad_maximum_fusion.refs_3_, ...), custom_call_target="tpu_custom_call" | custom-call | flops 851968 | bytes 3407872 | tf_op jit(solution)/shard_map/pallas_call | solution.py:121
  (33 shorter events, 1.1 us)
Async XLA Ops:
  0.6 2.0 %copy-start = (bf16[1,851968]{1,0:T(2,128)(2,1)S(1)}, bf16[1,851968]{1,0:T(2,128)(2,1)}, u32[]{:S(2)}) copy-start(bf16[1,851968]{1,0:T(2,128)(2,1)} %g_ref.3) | copy-start | bytes 5111812
  2.7 25.0 %copy-start.1 = (f32[26624]{0:T(1024)S(1)}, f32[26624]{0:T(1024)}, u32[]{:S(2)}) copy-start(f32[26624]{0:T(1024)} %param.7) | copy-start | bytes 319492
  2.7 25.0 %copy-start.2 = (f32[26624]{0:T(1024)S(1)}, f32[26624]{0:T(1024)}, u32[]{:S(2)}) copy-start(f32[26624]{0:T(1024)} %param.9) | copy-start | bytes 319492
  2.7 25.0 %copy-start.3 = (f32[26624]{0:T(1024)S(1)}, f32[26624]{0:T(1024)}, u32[]{:S(2)}) copy-start(f32[26624]{0:T(1024)} %param.8) | copy-start | bytes 319492
  2.9 7.1 %collective-permute-start = (bf16[2496,128]{1,0:T(8,128)(2,1)S(1)}, bf16[2496,128]{1,0:T(8,128)(2,1)S(1)}, u32[]{:S(2)}, u32[]{:S(2)}) collective-permute-start(bf16[2496,128]{1,0:T(8,128)(2,1)S(1)} %get-tuple-element.10), channel_id=1, source_target_pairs={{0,4},{4,0},{8,12},{12,8},{1,5},{5,1},{9,13},{13,9},{2,6},{6,2},{1... | collective-permute-start | bytes 1916936 | tf_op jit(solution)/shard_map/ppermute | solution.py:66
  3.5 2.0 %collective-permute-start.1 = (bf16[832,128]{1,0:T(8,128)(2,1)S(1)}, bf16[832,128]{1,0:T(8,128)(2,1)S(1)}, u32[]{:S(2)}, u32[]{:S(2)}) collective-permute-start(bf16[832,128]{1,0:T(8,128)(2,1)S(1)} %get-tuple-element.8.refs_0_), channel_id=1, source_target_pairs={{0,4},{4,0},{8,12},{12,8},{1,5},{5,1},{9,13},{13,9},{2,6},{6,2},{1... | collective-permute-start | bytes 638984 | tf_op jit(solution)/shard_map/ppermute | solution.py:66
  5.5 9.0 %collective-permute-start.2 = (bf16[416,128]{1,0:T(8,128)(2,1)S(1)}, bf16[416,128]{1,0:T(8,128)(2,1)S(1)}, u32[]{:S(2)}, u32[]{:S(2)}) collective-permute-start(bf16[416,128]{1,0:T(8,128)(2,1)S(1)} %get-tuple-element.21), channel_id=1, source_target_pairs={{0,1},{1,0},{2,3},{3,2},{4,5},{5,4},{6,7},{7,6},{8,9},{9,8},{10,11... | collective-permute-start | bytes 319496 | tf_op jit(solution)/shard_map/ppermute | solution.py:63
  8.5 7.6 %collective-permute-start.3 = (bf16[416,128]{1,0:T(8,128)(2,1)S(1)}, bf16[416,128]{1,0:T(8,128)(2,1)S(1)}, u32[]{:S(2)}, u32[]{:S(2)}) collective-permute-start(bf16[416,128]{1,0:T(8,128)(2,1)S(1)} %get-tuple-element.22), channel_id=1, source_target_pairs={{0,8},{1,9},{2,10},{3,11},{4,12},{5,13},{6,14},{7,15},{8,0},{9,1},... | collective-permute-start | bytes 319496 | tf_op jit(solution)/shard_map/ppermute | solution.py:63
  10.2 11.6 %collective-permute-start.4 = (bf16[416,128]{1,0:T(8,128)(2,1)S(1)}, bf16[416,128]{1,0:T(8,128)(2,1)S(1)}, u32[]{:S(2)}, u32[]{:S(2)}) collective-permute-start(bf16[416,128]{1,0:T(8,128)(2,1)S(1)} %get-tuple-element.16), channel_id=1, source_target_pairs={{0,16},{1,17},{2,18},{3,19},{4,20},{5,21},{6,22},{7,23},{8,24},{9,... | collective-permute-start | bytes 319496 | tf_op jit(solution)/shard_map/ppermute | solution.py:63
  11.7 10.0 %collective-permute-start.8 = (bf16[416,128]{1,0:T(8,128)(2,1)S(1)}, bf16[416,128]{1,0:T(8,128)(2,1)S(1)}, u32[]{:S(2)}, u32[]{:S(2)}) collective-permute-start(bf16[416,128]{1,0:T(8,128)(2,1)S(1)} %get-tuple-element.17), channel_id=1, source_target_pairs={{0,25},{1,24},{2,27},{3,26},{4,29},{5,28},{6,31},{7,30},{8,17},{9,... | collective-permute-start | bytes 319496 | tf_op jit(solution)/shard_map/ppermute | solution.py:63
  11.8 10.0 %collective-permute-start.7 = (bf16[416,128]{1,0:T(8,128)(2,1)S(1)}, bf16[416,128]{1,0:T(8,128)(2,1)S(1)}, u32[]{:S(2)}, u32[]{:S(2)}) collective-permute-start(bf16[416,128]{1,0:T(8,128)(2,1)S(1)} %get-tuple-element.18), channel_id=1, source_target_pairs={{0,24},{1,25},{2,26},{3,27},{4,28},{5,29},{6,30},{7,31},{8,16},{9,... | collective-permute-start | bytes 319496 | tf_op jit(solution)/shard_map/ppermute | solution.py:63
  14.6 7.2 %collective-permute-start.6 = (bf16[416,128]{1,0:T(8,128)(2,1)S(1)}, bf16[416,128]{1,0:T(8,128)(2,1)S(1)}, u32[]{:S(2)}, u32[]{:S(2)}) collective-permute-start(bf16[416,128]{1,0:T(8,128)(2,1)S(1)} %get-tuple-element.19), channel_id=1, source_target_pairs={{0,17},{1,16},{2,19},{3,18},{4,21},{5,20},{6,23},{7,22},{8,25},{9,... | collective-permute-start | bytes 319496 | tf_op jit(solution)/shard_map/ppermute | solution.py:63
  16.1 5.7 %collective-permute-start.5 = (bf16[416,128]{1,0:T(8,128)(2,1)S(1)}, bf16[416,128]{1,0:T(8,128)(2,1)S(1)}, u32[]{:S(2)}, u32[]{:S(2)}) collective-permute-start(bf16[416,128]{1,0:T(8,128)(2,1)S(1)} %get-tuple-element.20), channel_id=1, source_target_pairs={{0,9},{1,8},{2,11},{3,10},{4,13},{5,12},{6,15},{7,14},{8,1},{9,0},... | collective-permute-start | bytes 319496 | tf_op jit(solution)/shard_map/ppermute | solution.py:63
  22.0 5.7 %collective-permute-start.9 = (bf16[208,128]{1,0:T(8,128)(2,1)S(1)}, bf16[208,128]{1,0:T(8,128)(2,1)S(1)}, u32[]{:S(2)}, u32[]{:S(2)}) collective-permute-start(bf16[208,128]{1,0:T(8,128)(2,1)S(1)} %slice.107), channel_id=1, source_target_pairs={{0,2},{1,3},{2,0},{3,1},{4,6},{5,7},{6,4},{7,5},{8,10},{9,11},{10,... | collective-permute-start | bytes 159752 | tf_op jit(solution)/shard_map/ppermute | solution.py:63
  28.4 5.9 %collective-permute-start.12 = (bf16[208,128]{1,0:T(8,128)(2,1)S(1)}, bf16[208,128]{1,0:T(8,128)(2,1)S(1)}, u32[]{:S(2)}, u32[]{:S(2)}) collective-permute-start(bf16[208,128]{1,0:T(8,128)(2,1)S(1)} %get-tuple-element.12), channel_id=1, source_target_pairs={{0,3},{1,2},{2,1},{3,0},{4,7},{5,6},{6,5},{7,4},{8,11},{9,10},{10,... | collective-permute-start | bytes 159752 | tf_op jit(solution)/shard_map/ppermute | solution.py:63
  30.8 5.3 %collective-permute-start.11 = (bf16[208,128]{1,0:T(8,128)(2,1)S(1)}, bf16[208,128]{1,0:T(8,128)(2,1)S(1)}, u32[]{:S(2)}, u32[]{:S(2)}) collective-permute-start(bf16[208,128]{1,0:T(8,128)(2,1)S(1)} %get-tuple-element.12), channel_id=1, source_target_pairs={{0,2},{1,3},{2,0},{3,1},{4,6},{5,7},{6,4},{7,5},{8,10},{9,11},{10,... | collective-permute-start | bytes 159752 | tf_op jit(solution)/shard_map/ppermute | solution.py:63
  30.8 5.3 %collective-permute-start.10 = (bf16[208,128]{1,0:T(8,128)(2,1)S(1)}, bf16[208,128]{1,0:T(8,128)(2,1)S(1)}, u32[]{:S(2)}, u32[]{:S(2)}) collective-permute-start(bf16[208,128]{1,0:T(8,128)(2,1)S(1)} %get-tuple-element.12), channel_id=1, source_target_pairs={{0,1},{1,0},{2,3},{3,2},{4,5},{5,4},{6,7},{7,6},{8,9},{9,8},{10,11... | collective-permute-start | bytes 159752 | tf_op jit(solution)/shard_map/ppermute | solution.py:63
  36.1 6.9 %collective-permute-start.15 = (bf16[832,128]{1,0:T(8,128)(2,1)S(1)}, bf16[832,128]{1,0:T(8,128)(2,1)S(1)}, u32[]{:S(2)}, u32[]{:S(2)}) collective-permute-start(bf16[832,128]{1,0:T(8,128)(2,1)S(1)} %pad_maximum_fusion.refs_3_), channel_id=1, source_target_pairs={{0,24},{1,25},{2,26},{3,27},{4,28},{5,29},{6,30},{7,31},{8,16},{9,... | collective-permute-start | bytes 638984 | tf_op jit(solution)/shard_map/ppermute | solution.py:63
  38.4 6.8 %collective-permute-start.14 = (bf16[832,128]{1,0:T(8,128)(2,1)S(1)}, bf16[832,128]{1,0:T(8,128)(2,1)S(1)}, u32[]{:S(2)}, u32[]{:S(2)}) collective-permute-start(bf16[832,128]{1,0:T(8,128)(2,1)S(1)} %pad_maximum_fusion.refs_3_), channel_id=1, source_target_pairs={{0,16},{1,17},{2,18},{3,19},{4,20},{5,21},{6,22},{7,23},{8,24},{9,... | collective-permute-start | bytes 638984 | tf_op jit(solution)/shard_map/ppermute | solution.py:63
  38.6 6.6 %collective-permute-start.13 = (bf16[832,128]{1,0:T(8,128)(2,1)S(1)}, bf16[832,128]{1,0:T(8,128)(2,1)S(1)}, u32[]{:S(2)}, u32[]{:S(2)}) collective-permute-start(bf16[832,128]{1,0:T(8,128)(2,1)S(1)} %pad_maximum_fusion.refs_3_), channel_id=1, source_target_pairs={{0,8},{1,9},{2,10},{3,11},{4,12},{5,13},{6,14},{7,15},{8,0},{9,1},... | collective-permute-start | bytes 638984 | tf_op jit(solution)/shard_map/ppermute | solution.py:63
  39.6 6.1 %collective-permute-start.19 = (bf16[832,128]{1,0:T(8,128)(2,1)S(1)}, bf16[832,128]{1,0:T(8,128)(2,1)S(1)}, u32[]{:S(2)}, u32[]{:S(2)}) collective-permute-start(bf16[832,128]{1,0:T(8,128)(2,1)S(1)} %pad_maximum_fusion.refs_3_), channel_id=1, source_target_pairs={{0,4},{4,0},{8,12},{12,8},{1,5},{5,1},{9,13},{13,9},{2,6},{6,2},{1... | collective-permute-start | bytes 638984 | tf_op jit(solution)/shard_map/ppermute | solution.py:66
  43.0 2.7 %collective-permute-start.18 = (bf16[832,128]{1,0:T(8,128)(2,1)S(1)}, bf16[832,128]{1,0:T(8,128)(2,1)S(1)}, u32[]{:S(2)}, u32[]{:S(2)}) collective-permute-start(bf16[832,128]{1,0:T(8,128)(2,1)S(1)} %collective-permute-done.15.refs_2_), channel_id=1, source_target_pairs={{0,4},{4,0},{8,12},{12,8},{1,5},{5,1},{9,13},{13,9},{2,6},{6,2},{1... | collective-permute-start | bytes 638984 | tf_op jit(solution)/shard_map/ppermute | solution.py:66
  45.2 1.5 %collective-permute-start.17 = (bf16[832,128]{1,0:T(8,128)(2,1)S(1)}, bf16[832,128]{1,0:T(8,128)(2,1)S(1)}, u32[]{:S(2)}, u32[]{:S(2)}) collective-permute-start(bf16[832,128]{1,0:T(8,128)(2,1)S(1)} %collective-permute-done.14.refs_1_), channel_id=1, source_target_pairs={{0,4},{4,0},{8,12},{12,8},{1,5},{5,1},{9,13},{13,9},{2,6},{6,2},{1... | collective-permute-start | bytes 638984 | tf_op jit(solution)/shard_map/ppermute | solution.py:66
  45.2 1.7 %collective-permute-start.16 = (bf16[832,128]{1,0:T(8,128)(2,1)S(1)}, bf16[832,128]{1,0:T(8,128)(2,1)S(1)}, u32[]{:S(2)}, u32[]{:S(2)}) collective-permute-start(bf16[832,128]{1,0:T(8,128)(2,1)S(1)} %collective-permute-done.13.refs_0_), channel_id=1, source_target_pairs={{0,4},{4,0},{8,12},{12,8},{1,5},{5,1},{9,13},{13,9},{2,6},{6,2},{1... | collective-permute-start | bytes 638984 | tf_op jit(solution)/shard_map/ppermute | solution.py:66

commit v2 on v1

--- a/solution.py
+++ b/solution.py
@@ -13,10 +13,7 @@
 EPSILON = 1e-08
 LANES = 128
 VMEM_LIMIT = 8 << 20
-FIRST = 2
 X, PAIR, HIGH, LOW = range(4)
-SUM_STAGES = ((X, PAIR, LOW), (HIGH,))
-SPREAD_STAGES = ((HIGH, LOW), (X, PAIR))
 
 
 def adam_update(summed, master, first_moment, second_moment, step_count, step_size):
@@ -34,19 +31,26 @@
     def __init__(self):
         self.x, self.y, self.z = (lax.axis_size(a) for a in ("gx", "gy", "gz"))
         self.sizes = (self.x, self.y // 2, self.z // 2, 2)
+        self.square = self.sizes[:2] == (2, 2)
 
     def offsets(self, digits):
         every = itertools.product(*(range(n if i in digits else 1) for i, n in enumerate(self.sizes)))
         return sorted(every, key=lambda o: (not any(o), sum(v > 0 for v in o)))
 
+    def digits(self, offset, side):
+        if not self.square:
+            return offset
+        one, two = offset[:2]
+        return (two + side * (one - two), one + side * (two - one), *offset[2:])
+
     def block(self, sign, offset, other):
         at_x, at_y, at_z = (lax.axis_index(a) for a in ("gx", "gy", "gz"))
+        side = lax.rem(at_y, 2)
+        side = 1 - side if other else side
         place = (at_x, lax.div(at_y, 2), lax.div(at_z, 2), lax.rem(at_z, 2))
         x, pair, high, low = (
-            lax.rem(at + n + sign * o, n) if o else at for at, n, o in zip(place, self.sizes, offset)
+            lax.rem(at + n + sign * o, n) for at, n, o in zip(place, self.sizes, self.digits(offset, side))
         )
-        side = lax.rem(at_y, 2)
-        side = 1 - side if other else side
         return ((x * self.sizes[1] + pair) * 2 + side) * self.z + high * 2 + low
 
     def send(self, value, offset):
@@ -54,7 +58,7 @@
         for x, pair, side, high, low in itertools.product(
             *(range(n) for n in (*self.sizes[:2], 2, *self.sizes[2:]))
         ):
-            to = [(v + o) % n for v, o, n in zip((x, pair, high, low), offset, self.sizes)]
+            to = [(v + o) % n for v, o, n in zip((x, pair, high, low), self.digits(offset, side), self.sizes)]
             source, target = (
                 ((p[0] * self.sizes[1] + p[1]) * 2 + side) * self.z + p[2] * 2 + p[3]
                 for p in ((x, pair, high, low), to)
@@ -94,7 +98,7 @@
     )(gradients, *after)
 
 
-def place_blocks(pieces, held, block, total, places):
+def place_blocks(pieces, held, block, total, places, into=()):
     rows = block // LANES
     if rows % 8:
         where = jnp.stack([places.block(-1, *one) for one in held])
@@ -102,7 +106,7 @@
         return jnp.zeros_like(found).at[where].set(found).reshape(-1, LANES)
 
     def kernel(*refs):
-        sources, out_ref, sems = refs[: len(pieces)], refs[len(pieces)], refs[len(pieces) + 1]
+        sources, (out_ref, sems) = refs[: len(pieces)], refs[len(pieces) + len(into) :]
         copies = []
         for source in sources:
             for k in range(source.shape[0] // rows):
@@ -120,13 +124,14 @@
 
     return pl.pallas_call(
         kernel,
-        in_specs=[pl.BlockSpec(memory_space=pl.ANY)] * len(pieces),
+        in_specs=[pl.BlockSpec(memory_space=pl.ANY)] * (len(pieces) + len(into)),
         out_specs=pl.BlockSpec(memory_space=pl.ANY),
         out_shape=jax.ShapeDtypeStruct((total // LANES, LANES), pieces[0].dtype),
         scratch_shapes=[pltpu.SemaphoreType.DMA((len(held),))],
+        input_output_aliases={len(pieces): 0} if into else {},
         compiler_params=pltpu.CompilerParams(vmem_limit_bytes=VMEM_LIMIT),
         cost_estimate=pl.CostEstimate(flops=total, bytes_accessed=4 * total, transcendentals=0),
-    )(*pieces)
+    )(*pieces, *into)
 
 
 def per_device(gradients, master, first_moment, second_moment, step_count, step_size):
@@ -135,22 +140,30 @@
     rows = owned // LANES
     wide, narrow = jnp.float32, gradients.dtype
 
-    near, far = (places.offsets(digits) for digits in SUM_STAGES)
+    near, far = places.offsets((X, PAIR)), places.offsets((HIGH, LOW))
+    near = near[-2::-1] + near[-1:]
     size = len(far) * rows
-    arrived, after = [], []
-    for part in (near[:FIRST], near[FIRST:]):
+    values, after = {}, []
+    for part in (near[:1], near[2:3], near[1:2] + near[3:]):
         keep, send = dense_blocks(gradients, [both(o, f) for o in part for f in far], owned, places, after)
         after = [send]
         got = places.swap(send)
-        for slot, offset in enumerate(part):
+        for slot in range(len(part)):
             span = slice(slot * size, (slot + 1) * size)
-            value = keep[span].astype(wide) + got[span].astype(wide)
-            if any(offset):
-                arrived.append(places.send(value.astype(narrow), offset))
-            else:
-                total = value
-    for part in arrived:
-        total = total + part.astype(wide)
+            values[part[slot]] = keep[span].astype(wide) + got[span].astype(wide)
+
+    def plane_sent(value, offset):
+        return places.send(value.astype(narrow), offset).astype(wide)
+
+    total = values[near[-1]]
+    if places.square:
+        corner, second, first = near[:3]
+        passing = plane_sent(values[corner], first)
+        total = total + plane_sent(values[first], first)
+        total = total + plane_sent(values[second] + passing, second)
+    else:
+        for offset in near[:-1]:
+            total = total + plane_sent(values[offset], offset)
     moved = []
     for slot, offset in enumerate(far[:-1]):
         moved.append(places.send(total[slot * rows : (slot + 1) * rows].astype(narrow), offset))
@@ -158,22 +171,29 @@
     for part in moved:
         summed = summed + part.astype(wide)
 
-    new_master, new_first, new_second = adam_update(
-        summed.reshape(owned), master, first_moment, second_moment, step_count, step_size
-    )
-
-    far, near = (places.offsets(digits) for digits in SPREAD_STAGES)
-    line = [new_master.astype(narrow).reshape(rows, LANES)] * len(far)
+    state = (summed.reshape(owned), master, first_moment, second_moment, step_count, step_size)
+    block = adam_update(*state)[0].astype(narrow).reshape(rows, LANES)
+    new_master, new_first, new_second = adam_update(*lax.optimization_barrier(state))
+
+    line = [block] * len(far)
     for slot, offset in enumerate(far[:-1]):
         line[slot] = places.send(line[-1], offset)
     line = jnp.concatenate(line, axis=0)
-    pieces = [line] * len(near)
-    for slot, offset in enumerate(near[:-1]):
-        pieces[slot] = places.send(line, offset)
-    pieces = pieces + [places.swap(piece) for piece in pieces]
+
+    def plane_spread(value, offset):
+        return places.send(value, offset)
+
+    near = near[-2::-1] + near[-1:]
+    pieces = [plane_spread(line, offset) for offset in near[:-1]] + [line]
+    swapped = []
+    for piece in pieces:
+        swapped.append(places.swap(piece))
     held = [(both(o, f), other) for other in (False, True) for o in near for f in far]
-    weights = place_blocks(pieces, held, owned, gradients.shape[1], places)
-    return (new_master, new_first, new_second, weights.reshape(-1))
+    weights = ()
+    for part in (pieces, swapped) if rows % 8 == 0 else (pieces + swapped,):
+        weights = [place_blocks(part, held[: len(part) * len(far)], owned, gradients.shape[1], places, weights)]
+        held = held[len(part) * len(far) :]
+    return (new_master, new_first, new_second, weights[0].reshape(-1))
 
 
 def solution(mesh):

time: 48.6 us -> 47.8 us (0.984)
  starting transfers between devices: 22.2 us -> 18.3 us
  waiting for transfers between devices: 19.3 us -> 21.6 us
  Pallas kernels: 1.7 us -> 2.32 us
    ppermute x14 -> x12, waiting for transfers between devices: 16.1 us -> 21.3 us  [send(): return lax.ppermute(value, ('gx', 'gy', 'gz'), moves)]
    ppermute x14 -> x12, starting transfers between devices: 21.1 us -> 17 us  [send(): return lax.ppermute(value, ('gx', 'gy', 'gz'), moves)]
    ppermute x6 -> x7, waiting for transfers between devices: 3.18 us -> 0.28 us  [swap(): return lax.ppermute(value, 'gy', [(y, y ^ 1) for y in range(self.y)])]
    sub x0 -> x1, other arithmetic: none -> 0.75 us  [adam_update(): new_master = master - step_size[0] * update]
    reshape x1, other arithmetic: 0.76 us -> 0.12 us  [per_device(): block = adam_update(*state)[0].astype(narrow).reshape(rows, LANES)]
    pallas_call x1 -> x2, Pallas kernels: 1.44 us -> 2.08 us  [place_blocks(): pl.pallas_call(kernel, in_specs=[pl.BlockSpec(memory_space=pl.ANY)] * (le...]
    ppermute x6 -> x7, starting transfers between devices: 1.1 us -> 1.28 us  [swap(): return lax.ppermute(value, 'gy', [(y, y ^ 1) for y in range(self.y)])]
  transfers between devices with their start and end apart: 20 -> 19, of which waited for: 10 -> 12; matrix products, arithmetic and copies ran while one was open for 0% -> 2% of each run, Pallas kernels for 0% -> 3%
where the time goes in v2:
time: 47.8 us; the launch traced here: 47.6 us
  waiting for transfers between devices  21.6 us (45%)
  starting transfers between devices  18.3 us (38%)
  Pallas kernels  2.32 us (5%)
  between operations  2.25 us (5%)
  local copies, waits for them, and re-layouts  1.99 us (4%)
  other arithmetic  1.21 us (3%)
    ppermute x12, waiting for transfers between devices, send(): return lax.ppermute(value, ('gx', 'gy', 'gz'), moves)  21.3 us
    ppermute x12, starting transfers between devices, send(): return lax.ppermute(value, ('gx', 'gy', 'gz'), moves)  17 us
    pallas_call x2, Pallas kernels, place_blocks(): pl.pallas_call(kernel, in_specs=[pl.BlockSpec(memory_space=pl.ANY)] * (le...  2.08 us
    unnamed x8, local copies, waits for them, and re-layouts  1.98 us
    ppermute x7, starting transfers between devices, swap(): return lax.ppermute(value, 'gy', [(y, y ^ 1) for y in range(self.y)])  1.28 us
  transfers between devices with their start and end apart: 19, of which 12 were waited for; matrix products, arithmetic and copies ran while one was open for 2% of the time, Pallas kernels for 3%

profile of v2, /device:TPU:0, one launch (start us, length us, event | category | flops | bytes accessed | tf_op | source)
XLA Modules:
  0.0 47.6 jit_solution(3078314538880693897)
XLA Ops:
  0.6 2.0 %copy-done = bf16[1,851968]{1,0:T(2,128)(2,1)S(1)} copy-done((bf16[1,851968]{1,0:T(2,128)(2,1)S(1)}, bf16[1,851968]{1,0:T(2,128)(2,1)}, u32[]{:S(2)}) %copy-start) | copy-done | bytes 1703960
  2.7 0.6 %collective-permute-start.3 = (bf16[832,128]{1,0:T(8,128)(2,1)S(1)}, bf16[832,128]{1,0:T(8,128)(2,1)S(1)}, u32[]{:S(2)}, u32[]{:S(2)}) collective-permute-start(bf16[832,128]{1,0:T(8,128)(2,1)S(1)} %get-tuple-element.16.refs_0_), channel_id=1, source_target_pairs={{0,4},{4,0},{8,12},{12,8},{1,5},{5,1},{9,13},{13,9},{2,6},{6,2},{1... | collective-permute-start | bytes 638984 | tf_op jit(solution)/shard_map/ppermute | solution.py:70
  3.5 0.5 %collective-permute-start = (bf16[1664,128]{1,0:T(8,128)(2,1)S(1)}, bf16[1664,128]{1,0:T(8,128)(2,1)S(1)}, u32[]{:S(2)}, u32[]{:S(2)}) collective-permute-start(bf16[1664,128]{1,0:T(8,128)(2,1)S(1)} %get-tuple-element.19), channel_id=1, source_target_pairs={{0,4},{4,0},{8,12},{12,8},{1,5},{5,1},{9,13},{13,9},{2,6},{6,2},{1... | collective-permute-start | bytes 1277960 | tf_op jit(solution)/shard_map/ppermute | solution.py:70
  4.4 2.9 %collective-permute-start.4 = (bf16[832,128]{1,0:T(8,128)(2,1)S(1)}, bf16[832,128]{1,0:T(8,128)(2,1)S(1)}, u32[]{:S(2)}, u32[]{:S(2)}) collective-permute-start(bf16[832,128]{1,0:T(8,128)(2,1)S(1)} %add_convert_fusion.1), channel_id=1, source_target_pairs={{0,16},{1,17},{2,18},{3,19},{4,12},{5,13},{6,14},{7,15},{8,24},{9,... | collective-permute-start | bytes 638984 | tf_op jit(solution)/shard_map/ppermute | solution.py:67
  7.6 3.6 %collective-permute-done.4 = bf16[832,128]{1,0:T(8,128)(2,1)S(1)} collective-permute-done((bf16[832,128]{1,0:T(8,128)(2,1)S(1)}, bf16[832,128]{1,0:T(8,128)(2,1)S(1)}, u32[]{:S(2)}, u32[]{:S(2)}) %collective-permute-start.4) | collective-permute-done | bytes 213024 | tf_op jit(solution)/shard_map/ppermute | solution.py:67
  11.3 2.1 %collective-permute-start.5 = (bf16[832,128]{1,0:T(8,128)(2,1)S(1)}, bf16[832,128]{1,0:T(8,128)(2,1)S(1)}, u32[]{:S(2)}, u32[]{:S(2)}) collective-permute-start(bf16[832,128]{1,0:T(8,128)(2,1)S(1)} %add_convert_fusion), channel_id=1, source_target_pairs={{0,8},{1,9},{2,10},{3,11},{4,20},{5,21},{6,22},{7,23},{8,0},{9,1},... | collective-permute-start | bytes 638984 | tf_op jit(solution)/shard_map/ppermute | solution.py:67
  13.5 3.7 %collective-permute-done.5 = bf16[832,128]{1,0:T(8,128)(2,1)S(1)} collective-permute-done((bf16[832,128]{1,0:T(8,128)(2,1)S(1)}, bf16[832,128]{1,0:T(8,128)(2,1)S(1)}, u32[]{:S(2)}, u32[]{:S(2)}) %collective-permute-start.5) | collective-permute-done | bytes 213024 | tf_op jit(solution)/shard_map/ppermute | solution.py:67
  17.3 2.1 %collective-permute-start.6 = (bf16[208,128]{1,0:T(8,128)(2,1)S(1)}, bf16[208,128]{1,0:T(8,128)(2,1)S(1)}, u32[]{:S(2)}, u32[]{:S(2)}) collective-permute-start(bf16[208,128]{1,0:T(8,128)(2,1)S(1)} %get-tuple-element.35), channel_id=1, source_target_pairs={{0,1},{1,0},{2,3},{3,2},{4,5},{5,4},{6,7},{7,6},{8,9},{9,8},{10,11... | collective-permute-start | bytes 159752 | tf_op jit(solution)/shard_map/ppermute | solution.py:67
  19.5 2.6 %collective-permute-start.7 = (bf16[208,128]{1,0:T(8,128)(2,1)S(1)}, bf16[208,128]{1,0:T(8,128)(2,1)S(1)}, u32[]{:S(2)}, u32[]{:S(2)}) collective-permute-start(bf16[208,128]{1,0:T(8,128)(2,1)S(1)} %get-tuple-element.37), channel_id=1, source_target_pairs={{0,2},{1,3},{2,0},{3,1},{4,6},{5,7},{6,4},{7,5},{8,10},{9,11},{10,... | collective-permute-start | bytes 159752 | tf_op jit(solution)/shard_map/ppermute | solution.py:67
  23.4 2.2 %collective-permute-done.7 = bf16[208,128]{1,0:T(8,128)(2,1)S(1)} collective-permute-done((bf16[208,128]{1,0:T(8,128)(2,1)S(1)}, bf16[208,128]{1,0:T(8,128)(2,1)S(1)}, u32[]{:S(2)}, u32[]{:S(2)}) %collective-permute-start.7) | collective-permute-done | bytes 53280 | tf_op jit(solution)/shard_map/ppermute | solution.py:67
  25.6 2.9 %collective-permute-done.8 = bf16[208,128]{1,0:T(8,128)(2,1)S(1)} collective-permute-done((bf16[208,128]{1,0:T(8,128)(2,1)S(1)}, bf16[208,128]{1,0:T(8,128)(2,1)S(1)}, u32[]{:S(2)}, u32[]{:S(2)}) %collective-permute-start.8) | collective-permute-done | bytes 53280 | tf_op jit(solution)/shard_map/ppermute | solution.py:67
  28.8 0.6 %collective-permute-start.11 = (bf16[208,128]{1,0:T(8,128)(2,1)S(1)}, bf16[208,128]{1,0:T(8,128)(2,1)S(1)}, u32[]{:S(2)}, u32[]{:S(2)}) collective-permute-start(bf16[208,128]{1,0:T(8,128)(2,1)S(1)} %get-tuple-element.28), channel_id=1, source_target_pairs={{0,3},{1,2},{2,1},{3,0},{4,7},{5,6},{6,5},{7,4},{8,11},{9,10},{10,... | collective-permute-start | bytes 159752 | tf_op jit(solution)/shard_map/ppermute | solution.py:67
  29.3 2.9 %collective-permute-start.9 = (bf16[208,128]{1,0:T(8,128)(2,1)S(1)}, bf16[208,128]{1,0:T(8,128)(2,1)S(1)}, u32[]{:S(2)}, u32[]{:S(2)}) collective-permute-start(bf16[208,128]{1,0:T(8,128)(2,1)S(1)} %get-tuple-element.28), channel_id=1, source_target_pairs={{0,1},{1,0},{2,3},{3,2},{4,5},{5,4},{6,7},{7,6},{8,9},{9,8},{10,11... | collective-permute-start | bytes 159752 | tf_op jit(solution)/shard_map/ppermute | solution.py:67
  32.2 1.5 %collective-permute-done.10 = bf16[208,128]{1,0:T(8,128)(2,1)S(1)} collective-permute-done((bf16[208,128]{1,0:T(8,128)(2,1)S(1)}, bf16[208,128]{1,0:T(8,128)(2,1)S(1)}, u32[]{:S(2)}, u32[]{:S(2)}) %collective-permute-start.10) | collective-permute-done | bytes 53280 | tf_op jit(solution)/shard_map/ppermute | solution.py:67
  33.8 1.1 %collective-permute-done.11 = bf16[208,128]{1,0:T(8,128)(2,1)S(1)} collective-permute-done((bf16[208,128]{1,0:T(8,128)(2,1)S(1)}, bf16[208,128]{1,0:T(8,128)(2,1)S(1)}, u32[]{:S(2)}, u32[]{:S(2)}) %collective-permute-start.11) | collective-permute-done | bytes 53280 | tf_op jit(solution)/shard_map/ppermute | solution.py:67
  34.9 1.6 %collective-permute-start.12 = (bf16[832,128]{1,0:T(8,128)(2,1)S(1)}, bf16[832,128]{1,0:T(8,128)(2,1)S(1)}, u32[]{:S(2)}, u32[]{:S(2)}) collective-permute-start(bf16[832,128]{1,0:T(8,128)(2,1)S(1)} %pad_maximum_fusion.refs_3_), channel_id=1, source_target_pairs={{0,16},{1,17},{2,18},{3,19},{4,12},{5,13},{6,14},{7,15},{8,24},{9,... | collective-permute-start | bytes 638984 | tf_op jit(solution)/shard_map/ppermute | solution.py:67
  36.5 1.5 %collective-permute-start.14 = (bf16[832,128]{1,0:T(8,128)(2,1)S(1)}, bf16[832,128]{1,0:T(8,128)(2,1)S(1)}, u32[]{:S(2)}, u32[]{:S(2)}) collective-permute-start(bf16[832,128]{1,0:T(8,128)(2,1)S(1)} %pad_maximum_fusion.refs_3_), channel_id=1, source_target_pairs={{0,8},{1,9},{2,10},{3,11},{4,20},{5,21},{6,22},{7,23},{8,0},{9,1},... | collective-permute-start | bytes 638984 | tf_op jit(solution)/shard_map/ppermute | solution.py:67
  38.0 0.5 %collective-permute-start.16 = (bf16[832,128]{1,0:T(8,128)(2,1)S(1)}, bf16[832,128]{1,0:T(8,128)(2,1)S(1)}, u32[]{:S(2)}, u32[]{:S(2)}) collective-permute-start(bf16[832,128]{1,0:T(8,128)(2,1)S(1)} %pad_maximum_fusion.refs_3_), channel_id=1, source_target_pairs={{0,24},{1,25},{2,26},{3,27},{4,28},{5,29},{6,30},{7,31},{8,16},{9,... | collective-permute-start | bytes 638984 | tf_op jit(solution)/shard_map/ppermute | solution.py:67
  38.7 2.4 %collective-permute-done.12.refs_0_ = bf16[832,128]{1,0:T(8,128)(2,1)S(1)} collective-permute-done((bf16[832,128]{1,0:T(8,128)(2,1)S(1)}, bf16[832,128]{1,0:T(8,128)(2,1)S(1)}, u32[]{:S(2)}, u32[]{:S(2)}) %collective-permute-start.12) | collective-permute-done | bytes 213024 | tf_op jit(solution)/shard_map/ppermute | solution.py:67
  41.1 1.3 %collective-permute-done.14.refs_1_ = bf16[832,128]{1,0:T(8,128)(2,1)S(1)} collective-permute-done((bf16[832,128]{1,0:T(8,128)(2,1)S(1)}, bf16[832,128]{1,0:T(8,128)(2,1)S(1)}, u32[]{:S(2)}, u32[]{:S(2)}) %collective-permute-start.14) | collective-permute-done | bytes 213024 | tf_op jit(solution)/shard_map/ppermute | solution.py:67
  42.4 2.4 %collective-permute-done.16.refs_2_ = bf16[832,128]{1,0:T(8,128)(2,1)S(1)} collective-permute-done((bf16[832,128]{1,0:T(8,128)(2,1)S(1)}, bf16[832,128]{1,0:T(8,128)(2,1)S(1)}, u32[]{:S(2)}, u32[]{:S(2)}) %collective-permute-start.16) | collective-permute-done | bytes 213024 | tf_op jit(solution)/shard_map/ppermute | solution.py:67
  44.8 0.7 %multiply_subtract_fusion = (f32[26624]{0:T(1024)}, f32[26624]{0:T(1024)}, f32[26624]{0:T(1024)}) fusion(f32[26624]{0:T(1024)S(1)} %copy-done.1, f32[]{:T(128)} %bitcast.3, f32[]{:T(128)} %bitcast.2, f32[]{:T(128)} %bitcast.12, f32[26624]{0:T(1024)S(1)} %get-tuple-element.25, f32[26624]{0:T(1024)S(1)} %copy-done.2, f32[26624]{0:T(1024)S(1)} %copy-done.3), kind=kLoop, calls=%fused_computation.19 | loop fusion | flops 346112 | bytes 745484 | tf_op jit(solution)/shard_map/sub | solution.py:26
  45.5 1.0 %shard_map.96.refs_4_ = bf16[6656,128]{1,0:T(8,128)(2,1)} custom-call(bf16[832,128]{1,0:T(8,128)(2,1)S(1)} %collective-permute-done.12.refs_0_, bf16[832,128]{1,0:T(8,128)(2,1)S(1)} %collective-permute-done.14.refs_1_, bf16[832,128]{1,0:T(8,128)(2,1)S(1)} %collective-permute-done.16.refs_2_, bf16[832,128]{1,0:T(8,128)(2,1)S(1)} %pad_maximum_fusion.refs_3_), custom_call_target="tpu_custom_call" | custom-call | flops 851968 | bytes 3407872 | tf_op jit(solution)/shard_map/pallas_call | solution.py:125
  46.6 1.1 %shard_map.97 = bf16[6656,128]{1,0:T(8,128)(2,1)} custom-call(bf16[832,128]{1,0:T(8,128)(2,1)S(1)} %collective-permute-done.13.refs_0_, bf16[832,128]{1,0:T(8,128)(2,1)S(1)} %collective-permute-done.15.refs_1_, bf16[832,128]{1,0:T(8,128)(2,1)S(1)} %collective-permute-done.17.refs_2_, ...), custom_call_target="tpu_custom_call", output_to_operand_aliasing={{}: (4, {})} | custom-call | flops 851968 | bytes 3407872 | tf_op jit(solution)/shard_map/pallas_call | solution.py:125
  (35 shorter events, 1.7 us)
Async XLA Ops:
  0.6 2.0 %copy-start = (bf16[1,851968]{1,0:T(2,128)(2,1)S(1)}, bf16[1,851968]{1,0:T(2,128)(2,1)}, u32[]{:S(2)}) copy-start(bf16[1,851968]{1,0:T(2,128)(2,1)} %g_ref.5) | copy-start | bytes 5111812
  2.7 1.6 %collective-permute-start.3 = (bf16[832,128]{1,0:T(8,128)(2,1)S(1)}, bf16[832,128]{1,0:T(8,128)(2,1)S(1)}, u32[]{:S(2)}, u32[]{:S(2)}) collective-permute-start(bf16[832,128]{1,0:T(8,128)(2,1)S(1)} %get-tuple-element.16.refs_0_), channel_id=1, source_target_pairs={{0,4},{4,0},{8,12},{12,8},{1,5},{5,1},{9,13},{13,9},{2,6},{6,2},{1... | collective-permute-start | bytes 638984 | tf_op jit(solution)/shard_map/ppermute | solution.py:70
  3.3 4.1 %collective-permute-start.1 = (bf16[832,128]{1,0:T(8,128)(2,1)S(1)}, bf16[832,128]{1,0:T(8,128)(2,1)S(1)}, u32[]{:S(2)}, u32[]{:S(2)}) collective-permute-start(bf16[832,128]{1,0:T(8,128)(2,1)S(1)} %get-tuple-element.17.refs_0_), channel_id=1, source_target_pairs={{0,4},{4,0},{8,12},{12,8},{1,5},{5,1},{9,13},{13,9},{2,6},{6,2},{1... | collective-permute-start | bytes 638984 | tf_op jit(solution)/shard_map/ppermute | solution.py:70
  3.5 4.1 %collective-permute-start = (bf16[1664,128]{1,0:T(8,128)(2,1)S(1)}, bf16[1664,128]{1,0:T(8,128)(2,1)S(1)}, u32[]{:S(2)}, u32[]{:S(2)}) collective-permute-start(bf16[1664,128]{1,0:T(8,128)(2,1)S(1)} %get-tuple-element.19), channel_id=1, source_target_pairs={{0,4},{4,0},{8,12},{12,8},{1,5},{5,1},{9,13},{13,9},{2,6},{6,2},{1... | collective-permute-start | bytes 1277960 | tf_op jit(solution)/shard_map/ppermute | solution.py:70
  4.4 24.2 %copy-start.1 = (f32[26624]{0:T(1024)S(1)}, f32[26624]{0:T(1024)}, u32[]{:S(2)}) copy-start(f32[26624]{0:T(1024)} %param.7) | copy-start | bytes 319492
  4.4 24.2 %copy-start.2 = (f32[26624]{0:T(1024)S(1)}, f32[26624]{0:T(1024)}, u32[]{:S(2)}) copy-start(f32[26624]{0:T(1024)} %param.9) | copy-start | bytes 319492
  4.4 24.2 %copy-start.3 = (f32[26624]{0:T(1024)S(1)}, f32[26624]{0:T(1024)}, u32[]{:S(2)}) copy-start(f32[26624]{0:T(1024)} %param.8) | copy-start | bytes 319492
  4.4 6.8 %collective-permute-start.4 = (bf16[832,128]{1,0:T(8,128)(2,1)S(1)}, bf16[832,128]{1,0:T(8,128)(2,1)S(1)}, u32[]{:S(2)}, u32[]{:S(2)}) collective-permute-start(bf16[832,128]{1,0:T(8,128)(2,1)S(1)} %add_convert_fusion.1), channel_id=1, source_target_pairs={{0,16},{1,17},{2,18},{3,19},{4,12},{5,13},{6,14},{7,15},{8,24},{9,... | collective-permute-start | bytes 638984 | tf_op jit(solution)/shard_map/ppermute | solution.py:67
  7.4 6.0 %collective-permute-start.2 = (bf16[832,128]{1,0:T(8,128)(2,1)S(1)}, bf16[832,128]{1,0:T(8,128)(2,1)S(1)}, u32[]{:S(2)}, u32[]{:S(2)}) collective-permute-start(bf16[832,128]{1,0:T(8,128)(2,1)S(1)} %add_convert_fusion.2), channel_id=1, source_target_pairs={{0,16},{1,17},{2,18},{3,19},{4,12},{5,13},{6,14},{7,15},{8,24},{9,... | collective-permute-start | bytes 638984 | tf_op jit(solution)/shard_map/ppermute | solution.py:67
  11.3 5.9 %collective-permute-start.5 = (bf16[832,128]{1,0:T(8,128)(2,1)S(1)}, bf16[832,128]{1,0:T(8,128)(2,1)S(1)}, u32[]{:S(2)}, u32[]{:S(2)}) collective-permute-start(bf16[832,128]{1,0:T(8,128)(2,1)S(1)} %add_convert_fusion), channel_id=1, source_target_pairs={{0,8},{1,9},{2,10},{3,11},{4,20},{5,21},{6,22},{7,23},{8,0},{9,1},... | collective-permute-start | bytes 638984 | tf_op jit(solution)/shard_map/ppermute | solution.py:67
  17.3 6.1 %collective-permute-start.6 = (bf16[208,128]{1,0:T(8,128)(2,1)S(1)}, bf16[208,128]{1,0:T(8,128)(2,1)S(1)}, u32[]{:S(2)}, u32[]{:S(2)}) collective-permute-start(bf16[208,128]{1,0:T(8,128)(2,1)S(1)} %get-tuple-element.35), channel_id=1, source_target_pairs={{0,1},{1,0},{2,3},{3,2},{4,5},{5,4},{6,7},{7,6},{8,9},{9,8},{10,11... | collective-permute-start | bytes 159752 | tf_op jit(solution)/shard_map/ppermute | solution.py:67
  19.5 6.2 %collective-permute-start.7 = (bf16[208,128]{1,0:T(8,128)(2,1)S(1)}, bf16[208,128]{1,0:T(8,128)(2,1)S(1)}, u32[]{:S(2)}, u32[]{:S(2)}) collective-permute-start(bf16[208,128]{1,0:T(8,128)(2,1)S(1)} %get-tuple-element.37), channel_id=1, source_target_pairs={{0,2},{1,3},{2,0},{3,1},{4,6},{5,7},{6,4},{7,5},{8,10},{9,11},{10,... | collective-permute-start | bytes 159752 | tf_op jit(solution)/shard_map/ppermute | solution.py:67
  22.0 6.5 %collective-permute-start.8 = (bf16[208,128]{1,0:T(8,128)(2,1)S(1)}, bf16[208,128]{1,0:T(8,128)(2,1)S(1)}, u32[]{:S(2)}, u32[]{:S(2)}) collective-permute-start(bf16[208,128]{1,0:T(8,128)(2,1)S(1)} %get-tuple-element.36), channel_id=1, source_target_pairs={{0,3},{1,2},{2,1},{3,0},{4,7},{5,6},{6,5},{7,4},{8,11},{9,10},{10,... | collective-permute-start | bytes 159752 | tf_op jit(solution)/shard_map/ppermute | solution.py:67
  28.7 5.1 %collective-permute-start.10 = (bf16[208,128]{1,0:T(8,128)(2,1)S(1)}, bf16[208,128]{1,0:T(8,128)(2,1)S(1)}, u32[]{:S(2)}, u32[]{:S(2)}) collective-permute-start(bf16[208,128]{1,0:T(8,128)(2,1)S(1)} %get-tuple-element.28), channel_id=1, source_target_pairs={{0,2},{1,3},{2,0},{3,1},{4,6},{5,7},{6,4},{7,5},{8,10},{9,11},{10,... | collective-permute-start | bytes 159752 | tf_op jit(solution)/shard_map/ppermute | solution.py:67
  28.8 6.1 %collective-permute-start.11 = (bf16[208,128]{1,0:T(8,128)(2,1)S(1)}, bf16[208,128]{1,0:T(8,128)(2,1)S(1)}, u32[]{:S(2)}, u32[]{:S(2)}) collective-permute-start(bf16[208,128]{1,0:T(8,128)(2,1)S(1)} %get-tuple-element.28), channel_id=1, source_target_pairs={{0,3},{1,2},{2,1},{3,0},{4,7},{5,6},{6,5},{7,4},{8,11},{9,10},{10,... | collective-permute-start | bytes 159752 | tf_op jit(solution)/shard_map/ppermute | solution.py:67
  29.3 5.6 %collective-permute-start.9 = (bf16[208,128]{1,0:T(8,128)(2,1)S(1)}, bf16[208,128]{1,0:T(8,128)(2,1)S(1)}, u32[]{:S(2)}, u32[]{:S(2)}) collective-permute-start(bf16[208,128]{1,0:T(8,128)(2,1)S(1)} %get-tuple-element.28), channel_id=1, source_target_pairs={{0,1},{1,0},{2,3},{3,2},{4,5},{5,4},{6,7},{7,6},{8,9},{9,8},{10,11... | collective-permute-start | bytes 159752 | tf_op jit(solution)/shard_map/ppermute | solution.py:67
  34.9 6.1 %collective-permute-start.12 = (bf16[832,128]{1,0:T(8,128)(2,1)S(1)}, bf16[832,128]{1,0:T(8,128)(2,1)S(1)}, u32[]{:S(2)}, u32[]{:S(2)}) collective-permute-start(bf16[832,128]{1,0:T(8,128)(2,1)S(1)} %pad_maximum_fusion.refs_3_), channel_id=1, source_target_pairs={{0,16},{1,17},{2,18},{3,19},{4,12},{5,13},{6,14},{7,15},{8,24},{9,... | collective-permute-start | bytes 638984 | tf_op jit(solution)/shard_map/ppermute | solution.py:67
  36.5 5.8 %collective-permute-start.14 = (bf16[832,128]{1,0:T(8,128)(2,1)S(1)}, bf16[832,128]{1,0:T(8,128)(2,1)S(1)}, u32[]{:S(2)}, u32[]{:S(2)}) collective-permute-start(bf16[832,128]{1,0:T(8,128)(2,1)S(1)} %pad_maximum_fusion.refs_3_), channel_id=1, source_target_pairs={{0,8},{1,9},{2,10},{3,11},{4,20},{5,21},{6,22},{7,23},{8,0},{9,1},... | collective-permute-start | bytes 638984 | tf_op jit(solution)/shard_map/ppermute | solution.py:67
  38.0 6.7 %collective-permute-start.16 = (bf16[832,128]{1,0:T(8,128)(2,1)S(1)}, bf16[832,128]{1,0:T(8,128)(2,1)S(1)}, u32[]{:S(2)}, u32[]{:S(2)}) collective-permute-start(bf16[832,128]{1,0:T(8,128)(2,1)S(1)} %pad_maximum_fusion.refs_3_), channel_id=1, source_target_pairs={{0,24},{1,25},{2,26},{3,27},{4,28},{5,29},{6,30},{7,31},{8,16},{9,... | collective-permute-start | bytes 638984 | tf_op jit(solution)/shard_map/ppermute | solution.py:67
  38.6 8.0 %collective-permute-start.18 = (bf16[832,128]{1,0:T(8,128)(2,1)S(1)}, bf16[832,128]{1,0:T(8,128)(2,1)S(1)}, u32[]{:S(2)}, u32[]{:S(2)}) collective-permute-start(bf16[832,128]{1,0:T(8,128)(2,1)S(1)} %pad_maximum_fusion.refs_3_), channel_id=1, source_target_pairs={{0,4},{4,0},{8,12},{12,8},{1,5},{5,1},{9,13},{13,9},{2,6},{6,2},{1... | collective-permute-start | bytes 638984 | tf_op jit(solution)/shard_map/ppermute | solution.py:70
  41.1 5.5 %collective-permute-start.13 = (bf16[832,128]{1,0:T(8,128)(2,1)S(1)}, bf16[832,128]{1,0:T(8,128)(2,1)S(1)}, u32[]{:S(2)}, u32[]{:S(2)}) collective-permute-start(bf16[832,128]{1,0:T(8,128)(2,1)S(1)} %collective-permute-done.12.refs_0_), channel_id=1, source_target_pairs={{0,4},{4,0},{8,12},{12,8},{1,5},{5,1},{9,13},{13,9},{2,6},{6,2},{1... | collective-permute-start | bytes 638984 | tf_op jit(solution)/shard_map/ppermute | solution.py:70
  42.4 4.2 %collective-permute-start.15 = (bf16[832,128]{1,0:T(8,128)(2,1)S(1)}, bf16[832,128]{1,0:T(8,128)(2,1)S(1)}, u32[]{:S(2)}, u32[]{:S(2)}) collective-permute-start(bf16[832,128]{1,0:T(8,128)(2,1)S(1)} %collective-permute-done.14.refs_1_), channel_id=1, source_target_pairs={{0,4},{4,0},{8,12},{12,8},{1,5},{5,1},{9,13},{13,9},{2,6},{6,2},{1... | collective-permute-start | bytes 638984 | tf_op jit(solution)/shard_map/ppermute | solution.py:70
  44.8 1.8 %collective-permute-start.17 = (bf16[832,128]{1,0:T(8,128)(2,1)S(1)}, bf16[832,128]{1,0:T(8,128)(2,1)S(1)}, u32[]{:S(2)}, u32[]{:S(2)}) collective-permute-start(bf16[832,128]{1,0:T(8,128)(2,1)S(1)} %collective-permute-done.16.refs_2_), channel_id=1, source_target_pairs={{0,4},{4,0},{8,12},{12,8},{1,5},{5,1},{9,13},{13,9},{2,6},{6,2},{1... | collective-permute-start | bytes 638984 | tf_op jit(solution)/shard_map/ppermute | solution.py:70

commit v3 on v2

--- a/solution.py
+++ b/solution.py
@@ -142,6 +142,7 @@
 
     near, far = places.offsets((X, PAIR)), places.offsets((HIGH, LOW))
     near = near[-2::-1] + near[-1:]
+    far = far[1:-1] + far[:1] + far[-1:]
     size = len(far) * rows
     values, after = {}, []
     for part in (near[:1], near[2:3], near[1:2] + near[3:]):
@@ -159,14 +160,33 @@
     if places.square:
         corner, second, first = near[:3]
         passing = plane_sent(values[corner], first)
-        total = total + plane_sent(values[first], first)
-        total = total + plane_sent(values[second] + passing, second)
+        direct = plane_sent(values[first], first)
+        joined = values[second] + passing
+        half = size // 2
+        ahead = plane_sent(joined[:half], second)
+        behind = plane_sent(joined[half:], second)
+        total, direct, ahead = lax.optimization_barrier((total, direct, ahead))
+        total = total + direct
+        ahead = total[:half] + ahead
     else:
         for offset in near[:-1]:
             total = total + plane_sent(values[offset], offset)
+        half = 0
+        ahead, behind = total[:0], jnp.zeros_like(total)
     moved = []
-    for slot, offset in enumerate(far[:-1]):
-        moved.append(places.send(total[slot * rows : (slot + 1) * rows].astype(narrow), offset))
+
+    def line_sent(values, offsets):
+        for slot, offset in enumerate(offsets):
+            part = values[slot * rows : (slot + 1) * rows].astype(narrow)
+            moved.append((part, places.send(part, offset)))
+
+    count = half // rows
+    line_sent(ahead, far[:count])
+    if count:
+        *_, total, behind = lax.optimization_barrier((*(part for part, _ in moved), total, behind))
+    total = total[half:] + behind
+    line_sent(total, far[count:-1])
+    moved = [part for _, part in moved]
     summed = total[-rows:]
     for part in moved:
         summed = summed + part.astype(wide)
@@ -188,11 +208,16 @@
     swapped = []
     for piece in pieces:
         swapped.append(places.swap(piece))
-    held = [(both(o, f), other) for other in (False, True) for o in near for f in far]
+    held = [[(both(o, f), other) for f in far] for other in (False, True) for o in near]
+    pieces += swapped
+    last = [len(pieces) - 2] if rows % 8 == 0 else []
     weights = ()
-    for part in (pieces, swapped) if rows % 8 == 0 else (pieces + swapped,):
-        weights = [place_blocks(part, held[: len(part) * len(far)], owned, gradients.shape[1], places, weights)]
-        held = held[len(part) * len(far) :]
+    for part in ([k for k in range(len(pieces)) if k not in last], last):
+        if part:
+            blocks = sum((held[k] for k in part), [])
+            weights = [
+                place_blocks([pieces[k] for k in part], blocks, owned, gradients.shape[1], places, weights)
+            ]
     return (new_master, new_first, new_second, weights[0].reshape(-1))
 
 

time: 47.8 us -> 47.7 us (level)
    ppermute x12 -> x13, starting transfers between devices: 17 us -> 16.9 us  [send(): return lax.ppermute(value, ('gx', 'gy', 'gz'), moves)]
    ppermute x12 -> x13, waiting for transfers between devices: 21.3 us -> 21.2 us  [send(): return lax.ppermute(value, ('gx', 'gy', 'gz'), moves)]
  transfers between devices with their start and end apart: 19 -> 20, of which waited for: 12 -> 12; matrix products, arithmetic and copies ran while one was open for 2% -> 2% of each run, Pallas kernels for 3% -> 3%
where the time goes in v3:
time: 47.7 us; the launch traced here: 47.6 us
  waiting for transfers between devices  21.5 us (45%)
  starting transfers between devices  18.1 us (38%)
  Pallas kernels  2.35 us (5%)
  between operations  2.28 us (5%)
  local copies, waits for them, and re-layouts  2.01 us (4%)
  other arithmetic  1.31 us (3%)
    ppermute x13, waiting for transfers between devices, send(): return lax.ppermute(value, ('gx', 'gy', 'gz'), moves)  21.2 us
    ppermute x13, starting transfers between devices, send(): return lax.ppermute(value, ('gx', 'gy', 'gz'), moves)  16.9 us
    pallas_call x2, Pallas kernels, place_blocks(): pl.pallas_call(kernel, in_specs=[pl.BlockSpec(memory_space=pl.ANY)] * (le...  2.11 us
    unnamed x8, local copies, waits for them, and re-layouts  1.98 us
    ppermute x7, starting transfers between devices, swap(): return lax.ppermute(value, 'gy', [(y, y ^ 1) for y in range(self.y)])  1.28 us
  transfers between devices with their start and end apart: 20, of which 12 were waited for; matrix products, arithmetic and copies ran while one was open for 2% of the time, Pallas kernels for 3%

profile of v3, /device:TPU:0, one launch (start us, length us, event | category | flops | bytes accessed | tf_op | source)
XLA Modules:
  0.0 47.6 jit_solution(7889909834317085342)
XLA Ops:
  0.6 2.0 %copy-done = bf16[1,851968]{1,0:T(2,128)(2,1)S(1)} copy-done((bf16[1,851968]{1,0:T(2,128)(2,1)S(1)}, bf16[1,851968]{1,0:T(2,128)(2,1)}, u32[]{:S(2)}) %copy-start) | copy-done | bytes 1703960
  2.7 0.6 %collective-permute-start.3 = (bf16[832,128]{1,0:T(8,128)(2,1)S(1)}, bf16[832,128]{1,0:T(8,128)(2,1)S(1)}, u32[]{:S(2)}, u32[]{:S(2)}) collective-permute-start(bf16[832,128]{1,0:T(8,128)(2,1)S(1)} %get-tuple-element.21.refs_0_), channel_id=1, source_target_pairs={{0,4},{4,0},{8,12},{12,8},{1,5},{5,1},{9,13},{13,9},{2,6},{6,2},{1... | collective-permute-start | bytes 638984 | tf_op jit(solution)/shard_map/ppermute | solution.py:70
  4.4 2.9 %collective-permute-start.4 = (bf16[832,128]{1,0:T(8,128)(2,1)S(1)}, bf16[832,128]{1,0:T(8,128)(2,1)S(1)}, u32[]{:S(2)}, u32[]{:S(2)}) collective-permute-start(bf16[832,128]{1,0:T(8,128)(2,1)S(1)} %add_convert_fusion.1), channel_id=1, source_target_pairs={{0,16},{1,17},{2,18},{3,19},{4,12},{5,13},{6,14},{7,15},{8,24},{9,... | collective-permute-start | bytes 638984 | tf_op jit(solution)/shard_map/ppermute | solution.py:67
  7.6 3.5 %collective-permute-done.4 = bf16[832,128]{1,0:T(8,128)(2,1)S(1)} collective-permute-done((bf16[832,128]{1,0:T(8,128)(2,1)S(1)}, bf16[832,128]{1,0:T(8,128)(2,1)S(1)}, u32[]{:S(2)}, u32[]{:S(2)}) %collective-permute-start.4) | collective-permute-done | bytes 213024 | tf_op jit(solution)/shard_map/ppermute | solution.py:67
  11.3 2.1 %collective-permute-start.5 = (bf16[416,128]{1,0:T(8,128)(2,1)S(1)}, bf16[416,128]{1,0:T(8,128)(2,1)S(1)}, u32[]{:S(2)}, u32[]{:S(2)}) collective-permute-start(bf16[416,128]{1,0:T(8,128)(2,1)S(1)} %get-tuple-element.46), channel_id=1, source_target_pairs={{0,8},{1,9},{2,10},{3,11},{4,20},{5,21},{6,22},{7,23},{8,0},{9,1},... | collective-permute-start | bytes 319496 | tf_op jit(solution)/shard_map/ppermute | solution.py:67
  13.5 2.6 %collective-permute-done.5 = bf16[416,128]{1,0:T(8,128)(2,1)S(1)} collective-permute-done((bf16[416,128]{1,0:T(8,128)(2,1)S(1)}, bf16[416,128]{1,0:T(8,128)(2,1)S(1)}, u32[]{:S(2)}, u32[]{:S(2)}) %collective-permute-start.5) | collective-permute-done | bytes 106528 | tf_op jit(solution)/shard_map/ppermute | solution.py:67
  16.2 1.9 %collective-permute-done.6 = bf16[416,128]{1,0:T(8,128)(2,1)S(1)} collective-permute-done((bf16[416,128]{1,0:T(8,128)(2,1)S(1)}, bf16[416,128]{1,0:T(8,128)(2,1)S(1)}, u32[]{:S(2)}, u32[]{:S(2)}) %collective-permute-start.6) | collective-permute-done | bytes 106528 | tf_op jit(solution)/shard_map/ppermute | solution.py:67
  18.1 1.6 %collective-permute-start.9 = (bf16[208,128]{1,0:T(8,128)(2,1)S(1)}, bf16[208,128]{1,0:T(8,128)(2,1)S(1)}, u32[]{:S(2)}, u32[]{:S(2)}) collective-permute-start(bf16[208,128]{1,0:T(8,128)(2,1)S(1)} %slice.78), channel_id=1, source_target_pairs={{0,1},{1,0},{2,3},{3,2},{4,5},{5,4},{6,7},{7,6},{8,9},{9,8},{10,11... | collective-permute-start | bytes 159752 | tf_op jit(solution)/shard_map/ppermute | solution.py:67
  19.8 2.6 %collective-permute-start.7 = (bf16[208,128]{1,0:T(8,128)(2,1)S(1)}, bf16[208,128]{1,0:T(8,128)(2,1)S(1)}, u32[]{:S(2)}, u32[]{:S(2)}) collective-permute-start(bf16[208,128]{1,0:T(8,128)(2,1)S(1)} %get-tuple-element.48), channel_id=1, source_target_pairs={{0,2},{1,3},{2,0},{3,1},{4,6},{5,7},{6,4},{7,5},{8,10},{9,11},{10,... | collective-permute-start | bytes 159752 | tf_op jit(solution)/shard_map/ppermute | solution.py:67
  24.0 2.0 %collective-permute-done.7 = bf16[208,128]{1,0:T(8,128)(2,1)S(1)} collective-permute-done((bf16[208,128]{1,0:T(8,128)(2,1)S(1)}, bf16[208,128]{1,0:T(8,128)(2,1)S(1)}, u32[]{:S(2)}, u32[]{:S(2)}) %collective-permute-start.7) | collective-permute-done | bytes 53280 | tf_op jit(solution)/shard_map/ppermute | solution.py:67
  25.9 2.6 %collective-permute-done.8 = bf16[208,128]{1,0:T(8,128)(2,1)S(1)} collective-permute-done((bf16[208,128]{1,0:T(8,128)(2,1)S(1)}, bf16[208,128]{1,0:T(8,128)(2,1)S(1)}, u32[]{:S(2)}, u32[]{:S(2)}) %collective-permute-start.8) | collective-permute-done | bytes 53280 | tf_op jit(solution)/shard_map/ppermute | solution.py:67
  28.7 0.9 %collective-permute-start.11 = (bf16[208,128]{1,0:T(8,128)(2,1)S(1)}, bf16[208,128]{1,0:T(8,128)(2,1)S(1)}, u32[]{:S(2)}, u32[]{:S(2)}) collective-permute-start(bf16[208,128]{1,0:T(8,128)(2,1)S(1)} %get-tuple-element.38), channel_id=1, source_target_pairs={{0,3},{1,2},{2,1},{3,0},{4,7},{5,6},{6,5},{7,4},{8,11},{9,10},{10,... | collective-permute-start | bytes 159752 | tf_op jit(solution)/shard_map/ppermute | solution.py:67
  29.6 2.6 %collective-permute-start.12 = (bf16[208,128]{1,0:T(8,128)(2,1)S(1)}, bf16[208,128]{1,0:T(8,128)(2,1)S(1)}, u32[]{:S(2)}, u32[]{:S(2)}) collective-permute-start(bf16[208,128]{1,0:T(8,128)(2,1)S(1)} %get-tuple-element.38), channel_id=1, source_target_pairs={{0,1},{1,0},{2,3},{3,2},{4,5},{5,4},{6,7},{7,6},{8,9},{9,8},{10,11... | collective-permute-start | bytes 159752 | tf_op jit(solution)/shard_map/ppermute | solution.py:67
  32.2 1.5 %collective-permute-done.10 = bf16[208,128]{1,0:T(8,128)(2,1)S(1)} collective-permute-done((bf16[208,128]{1,0:T(8,128)(2,1)S(1)}, bf16[208,128]{1,0:T(8,128)(2,1)S(1)}, u32[]{:S(2)}, u32[]{:S(2)}) %collective-permute-start.10) | collective-permute-done | bytes 53280 | tf_op jit(solution)/shard_map/ppermute | solution.py:67
  33.7 1.1 %collective-permute-done.11 = bf16[208,128]{1,0:T(8,128)(2,1)S(1)} collective-permute-done((bf16[208,128]{1,0:T(8,128)(2,1)S(1)}, bf16[208,128]{1,0:T(8,128)(2,1)S(1)}, u32[]{:S(2)}, u32[]{:S(2)}) %collective-permute-start.11) | collective-permute-done | bytes 53280 | tf_op jit(solution)/shard_map/ppermute | solution.py:67
  34.9 1.6 %collective-permute-start.15 = (bf16[832,128]{1,0:T(8,128)(2,1)S(1)}, bf16[832,128]{1,0:T(8,128)(2,1)S(1)}, u32[]{:S(2)}, u32[]{:S(2)}) collective-permute-start(bf16[832,128]{1,0:T(8,128)(2,1)S(1)} %pad_maximum_fusion.refs_3_), channel_id=1, source_target_pairs={{0,16},{1,17},{2,18},{3,19},{4,12},{5,13},{6,14},{7,15},{8,24},{9,... | collective-permute-start | bytes 638984 | tf_op jit(solution)/shard_map/ppermute | solution.py:67
  36.5 1.4 %collective-permute-start.16 = (bf16[832,128]{1,0:T(8,128)(2,1)S(1)}, bf16[832,128]{1,0:T(8,128)(2,1)S(1)}, u32[]{:S(2)}, u32[]{:S(2)}) collective-permute-start(bf16[832,128]{1,0:T(8,128)(2,1)S(1)} %pad_maximum_fusion.refs_3_), channel_id=1, source_target_pairs={{0,8},{1,9},{2,10},{3,11},{4,20},{5,21},{6,22},{7,23},{8,0},{9,1},... | collective-permute-start | bytes 638984 | tf_op jit(solution)/shard_map/ppermute | solution.py:67
  37.9 0.5 %collective-permute-start.13 = (bf16[832,128]{1,0:T(8,128)(2,1)S(1)}, bf16[832,128]{1,0:T(8,128)(2,1)S(1)}, u32[]{:S(2)}, u32[]{:S(2)}) collective-permute-start(bf16[832,128]{1,0:T(8,128)(2,1)S(1)} %pad_maximum_fusion.refs_3_), channel_id=1, source_target_pairs={{0,24},{1,25},{2,26},{3,27},{4,28},{5,29},{6,30},{7,31},{8,16},{9,... | collective-permute-start | bytes 638984 | tf_op jit(solution)/shard_map/ppermute | solution.py:67
  38.6 2.5 %collective-permute-done.15.refs_0_ = bf16[832,128]{1,0:T(8,128)(2,1)S(1)} collective-permute-done((bf16[832,128]{1,0:T(8,128)(2,1)S(1)}, bf16[832,128]{1,0:T(8,128)(2,1)S(1)}, u32[]{:S(2)}, u32[]{:S(2)}) %collective-permute-start.15) | collective-permute-done | bytes 213024 | tf_op jit(solution)/shard_map/ppermute | solution.py:67
  41.1 1.2 %collective-permute-done.16.refs_1_ = bf16[832,128]{1,0:T(8,128)(2,1)S(1)} collective-permute-done((bf16[832,128]{1,0:T(8,128)(2,1)S(1)}, bf16[832,128]{1,0:T(8,128)(2,1)S(1)}, u32[]{:S(2)}, u32[]{:S(2)}) %collective-permute-start.16) | collective-permute-done | bytes 213024 | tf_op jit(solution)/shard_map/ppermute | solution.py:67
  42.3 2.3 %collective-permute-done.13.refs_2_ = bf16[832,128]{1,0:T(8,128)(2,1)S(1)} collective-permute-done((bf16[832,128]{1,0:T(8,128)(2,1)S(1)}, bf16[832,128]{1,0:T(8,128)(2,1)S(1)}, u32[]{:S(2)}, u32[]{:S(2)}) %collective-permute-start.13) | collective-permute-done | bytes 213024 | tf_op jit(solution)/shard_map/ppermute | solution.py:67
  44.7 0.7 %multiply_subtract_fusion = (f32[26624]{0:T(1024)}, f32[26624]{0:T(1024)}, f32[26624]{0:T(1024)}) fusion(f32[26624]{0:T(1024)S(1)} %copy-done.1, f32[]{:T(128)} %bitcast.3, f32[]{:T(128)} %bitcast.2, f32[]{:T(128)} %bitcast.12, f32[26624]{0:T(1024)S(1)} %get-tuple-element.35, f32[26624]{0:T(1024)S(1)} %copy-done.2, f32[26624]{0:T(1024)S(1)} %copy-done.3), kind=kLoop, calls=%fused_computation.23 | loop fusion | flops 346112 | bytes 745484 | tf_op jit(solution)/shard_map/sub | solution.py:26
  45.4 1.4 %shard_map.96.refs_1_ = bf16[6656,128]{1,0:T(8,128)(2,1)} custom-call(bf16[832,128]{1,0:T(8,128)(2,1)S(1)} %collective-permute-done.15.refs_0_, bf16[832,128]{1,0:T(8,128)(2,1)S(1)} %collective-permute-done.16.refs_1_, bf16[832,128]{1,0:T(8,128)(2,1)S(1)} %collective-permute-done.13.refs_2_, bf16[832,128]{1,0:T(8,128)(2,1)S(1)} %pad_maximum_fusion.refs_3_, ...), custom_call_target="tpu_custom_call" | custom-call | flops 851968 | bytes 3407872 | tf_op jit(solution)/shard_map/pallas_call | solution.py:125
  46.8 0.7 %shard_map.97 = bf16[6656,128]{1,0:T(8,128)(2,1)} custom-call(bf16[832,128]{1,0:T(8,128)(2,1)S(1)} %collective-permute-done.14.refs_0_, bf16[6656,128]{1,0:T(8,128)(2,1)} %shard_map.96.refs_1_), custom_call_target="tpu_custom_call", output_to_operand_aliasing={{}: (1, {})} | custom-call | flops 851968 | bytes 3407872 | tf_op jit(solution)/shard_map/pallas_call | solution.py:125
  (44 shorter events, 2.5 us)
Async XLA Ops:
  0.6 2.0 %copy-start = (bf16[1,851968]{1,0:T(2,128)(2,1)S(1)}, bf16[1,851968]{1,0:T(2,128)(2,1)}, u32[]{:S(2)}) copy-start(bf16[1,851968]{1,0:T(2,128)(2,1)} %g_ref.5) | copy-start | bytes 5111812
  2.7 1.6 %collective-permute-start.3 = (bf16[832,128]{1,0:T(8,128)(2,1)S(1)}, bf16[832,128]{1,0:T(8,128)(2,1)S(1)}, u32[]{:S(2)}, u32[]{:S(2)}) collective-permute-start(bf16[832,128]{1,0:T(8,128)(2,1)S(1)} %get-tuple-element.21.refs_0_), channel_id=1, source_target_pairs={{0,4},{4,0},{8,12},{12,8},{1,5},{5,1},{9,13},{13,9},{2,6},{6,2},{1... | collective-permute-start | bytes 638984 | tf_op jit(solution)/shard_map/ppermute | solution.py:70
  3.3 4.0 %collective-permute-start.1 = (bf16[832,128]{1,0:T(8,128)(2,1)S(1)}, bf16[832,128]{1,0:T(8,128)(2,1)S(1)}, u32[]{:S(2)}, u32[]{:S(2)}) collective-permute-start(bf16[832,128]{1,0:T(8,128)(2,1)S(1)} %get-tuple-element.22.refs_0_), channel_id=1, source_target_pairs={{0,4},{4,0},{8,12},{12,8},{1,5},{5,1},{9,13},{13,9},{2,6},{6,2},{1... | collective-permute-start | bytes 638984 | tf_op jit(solution)/shard_map/ppermute | solution.py:70
  3.5 4.1 %collective-permute-start = (bf16[1664,128]{1,0:T(8,128)(2,1)S(1)}, bf16[1664,128]{1,0:T(8,128)(2,1)S(1)}, u32[]{:S(2)}, u32[]{:S(2)}) collective-permute-start(bf16[1664,128]{1,0:T(8,128)(2,1)S(1)} %get-tuple-element.24), channel_id=1, source_target_pairs={{0,4},{4,0},{8,12},{12,8},{1,5},{5,1},{9,13},{13,9},{2,6},{6,2},{1... | collective-permute-start | bytes 1277960 | tf_op jit(solution)/shard_map/ppermute | solution.py:70
  4.4 6.8 %collective-permute-start.4 = (bf16[832,128]{1,0:T(8,128)(2,1)S(1)}, bf16[832,128]{1,0:T(8,128)(2,1)S(1)}, u32[]{:S(2)}, u32[]{:S(2)}) collective-permute-start(bf16[832,128]{1,0:T(8,128)(2,1)S(1)} %add_convert_fusion.1), channel_id=1, source_target_pairs={{0,16},{1,17},{2,18},{3,19},{4,12},{5,13},{6,14},{7,15},{8,24},{9,... | collective-permute-start | bytes 638984 | tf_op jit(solution)/shard_map/ppermute | solution.py:67
  7.4 6.1 %collective-permute-start.2 = (bf16[832,128]{1,0:T(8,128)(2,1)S(1)}, bf16[832,128]{1,0:T(8,128)(2,1)S(1)}, u32[]{:S(2)}, u32[]{:S(2)}) collective-permute-start(bf16[832,128]{1,0:T(8,128)(2,1)S(1)} %add_convert_fusion.2), channel_id=1, source_target_pairs={{0,16},{1,17},{2,18},{3,19},{4,12},{5,13},{6,14},{7,15},{8,24},{9,... | collective-permute-start | bytes 638984 | tf_op jit(solution)/shard_map/ppermute | solution.py:67
  11.3 4.8 %collective-permute-start.5 = (bf16[416,128]{1,0:T(8,128)(2,1)S(1)}, bf16[416,128]{1,0:T(8,128)(2,1)S(1)}, u32[]{:S(2)}, u32[]{:S(2)}) collective-permute-start(bf16[416,128]{1,0:T(8,128)(2,1)S(1)} %get-tuple-element.46), channel_id=1, source_target_pairs={{0,8},{1,9},{2,10},{3,11},{4,20},{5,21},{6,22},{7,23},{8,0},{9,1},... | collective-permute-start | bytes 319496 | tf_op jit(solution)/shard_map/ppermute | solution.py:67
  13.3 4.7 %collective-permute-start.6 = (bf16[416,128]{1,0:T(8,128)(2,1)S(1)}, bf16[416,128]{1,0:T(8,128)(2,1)S(1)}, u32[]{:S(2)}, u32[]{:S(2)}) collective-permute-start(bf16[416,128]{1,0:T(8,128)(2,1)S(1)} %get-tuple-element.45), channel_id=1, source_target_pairs={{0,8},{1,9},{2,10},{3,11},{4,20},{5,21},{6,22},{7,23},{8,0},{9,1},... | collective-permute-start | bytes 319496 | tf_op jit(solution)/shard_map/ppermute | solution.py:67
  13.5 15.0 %copy-start.1 = (f32[26624]{0:T(1024)S(1)}, f32[26624]{0:T(1024)}, u32[]{:S(2)}) copy-start(f32[26624]{0:T(1024)} %param.7) | copy-start | bytes 319492
  13.5 15.0 %copy-start.2 = (f32[26624]{0:T(1024)S(1)}, f32[26624]{0:T(1024)}, u32[]{:S(2)}) copy-start(f32[26624]{0:T(1024)} %param.9) | copy-start | bytes 319492
  13.5 15.0 %copy-start.3 = (f32[26624]{0:T(1024)S(1)}, f32[26624]{0:T(1024)}, u32[]{:S(2)}) copy-start(f32[26624]{0:T(1024)} %param.8) | copy-start | bytes 319492
  18.1 5.8 %collective-permute-start.9 = (bf16[208,128]{1,0:T(8,128)(2,1)S(1)}, bf16[208,128]{1,0:T(8,128)(2,1)S(1)}, u32[]{:S(2)}, u32[]{:S(2)}) collective-permute-start(bf16[208,128]{1,0:T(8,128)(2,1)S(1)} %slice.78), channel_id=1, source_target_pairs={{0,1},{1,0},{2,3},{3,2},{4,5},{5,4},{6,7},{7,6},{8,9},{9,8},{10,11... | collective-permute-start | bytes 159752 | tf_op jit(solution)/shard_map/ppermute | solution.py:67
  19.8 6.2 %collective-permute-start.7 = (bf16[208,128]{1,0:T(8,128)(2,1)S(1)}, bf16[208,128]{1,0:T(8,128)(2,1)S(1)}, u32[]{:S(2)}, u32[]{:S(2)}) collective-permute-start(bf16[208,128]{1,0:T(8,128)(2,1)S(1)} %get-tuple-element.48), channel_id=1, source_target_pairs={{0,2},{1,3},{2,0},{3,1},{4,6},{5,7},{6,4},{7,5},{8,10},{9,11},{10,... | collective-permute-start | bytes 159752 | tf_op jit(solution)/shard_map/ppermute | solution.py:67
  22.4 6.2 %collective-permute-start.8 = (bf16[208,128]{1,0:T(8,128)(2,1)S(1)}, bf16[208,128]{1,0:T(8,128)(2,1)S(1)}, u32[]{:S(2)}, u32[]{:S(2)}) collective-permute-start(bf16[208,128]{1,0:T(8,128)(2,1)S(1)} %get-tuple-element.47), channel_id=1, source_target_pairs={{0,3},{1,2},{2,1},{3,0},{4,7},{5,6},{6,5},{7,4},{8,11},{9,10},{10,... | collective-permute-start | bytes 159752 | tf_op jit(solution)/shard_map/ppermute | solution.py:67
  28.6 5.1 %collective-permute-start.10 = (bf16[208,128]{1,0:T(8,128)(2,1)S(1)}, bf16[208,128]{1,0:T(8,128)(2,1)S(1)}, u32[]{:S(2)}, u32[]{:S(2)}) collective-permute-start(bf16[208,128]{1,0:T(8,128)(2,1)S(1)} %get-tuple-element.38), channel_id=1, source_target_pairs={{0,2},{1,3},{2,0},{3,1},{4,6},{5,7},{6,4},{7,5},{8,10},{9,11},{10,... | collective-permute-start | bytes 159752 | tf_op jit(solution)/shard_map/ppermute | solution.py:67
  28.7 6.1 %collective-permute-start.11 = (bf16[208,128]{1,0:T(8,128)(2,1)S(1)}, bf16[208,128]{1,0:T(8,128)(2,1)S(1)}, u32[]{:S(2)}, u32[]{:S(2)}) collective-permute-start(bf16[208,128]{1,0:T(8,128)(2,1)S(1)} %get-tuple-element.38), channel_id=1, source_target_pairs={{0,3},{1,2},{2,1},{3,0},{4,7},{5,6},{6,5},{7,4},{8,11},{9,10},{10,... | collective-permute-start | bytes 159752 | tf_op jit(solution)/shard_map/ppermute | solution.py:67
  29.6 5.2 %collective-permute-start.12 = (bf16[208,128]{1,0:T(8,128)(2,1)S(1)}, bf16[208,128]{1,0:T(8,128)(2,1)S(1)}, u32[]{:S(2)}, u32[]{:S(2)}) collective-permute-start(bf16[208,128]{1,0:T(8,128)(2,1)S(1)} %get-tuple-element.38), channel_id=1, source_target_pairs={{0,1},{1,0},{2,3},{3,2},{4,5},{5,4},{6,7},{7,6},{8,9},{9,8},{10,11... | collective-permute-start | bytes 159752 | tf_op jit(solution)/shard_map/ppermute | solution.py:67
  34.9 6.2 %collective-permute-start.15 = (bf16[832,128]{1,0:T(8,128)(2,1)S(1)}, bf16[832,128]{1,0:T(8,128)(2,1)S(1)}, u32[]{:S(2)}, u32[]{:S(2)}) collective-permute-start(bf16[832,128]{1,0:T(8,128)(2,1)S(1)} %pad_maximum_fusion.refs_3_), channel_id=1, source_target_pairs={{0,16},{1,17},{2,18},{3,19},{4,12},{5,13},{6,14},{7,15},{8,24},{9,... | collective-permute-start | bytes 638984 | tf_op jit(solution)/shard_map/ppermute | solution.py:67
  36.5 5.8 %collective-permute-start.16 = (bf16[832,128]{1,0:T(8,128)(2,1)S(1)}, bf16[832,128]{1,0:T(8,128)(2,1)S(1)}, u32[]{:S(2)}, u32[]{:S(2)}) collective-permute-start(bf16[832,128]{1,0:T(8,128)(2,1)S(1)} %pad_maximum_fusion.refs_3_), channel_id=1, source_target_pairs={{0,8},{1,9},{2,10},{3,11},{4,20},{5,21},{6,22},{7,23},{8,0},{9,1},... | collective-permute-start | bytes 638984 | tf_op jit(solution)/shard_map/ppermute | solution.py:67
  37.9 6.7 %collective-permute-start.13 = (bf16[832,128]{1,0:T(8,128)(2,1)S(1)}, bf16[832,128]{1,0:T(8,128)(2,1)S(1)}, u32[]{:S(2)}, u32[]{:S(2)}) collective-permute-start(bf16[832,128]{1,0:T(8,128)(2,1)S(1)} %pad_maximum_fusion.refs_3_), channel_id=1, source_target_pairs={{0,24},{1,25},{2,26},{3,27},{4,28},{5,29},{6,30},{7,31},{8,16},{9,... | collective-permute-start | bytes 638984 | tf_op jit(solution)/shard_map/ppermute | solution.py:67
  38.5 6.9 %collective-permute-start.19 = (bf16[832,128]{1,0:T(8,128)(2,1)S(1)}, bf16[832,128]{1,0:T(8,128)(2,1)S(1)}, u32[]{:S(2)}, u32[]{:S(2)}) collective-permute-start(bf16[832,128]{1,0:T(8,128)(2,1)S(1)} %pad_maximum_fusion.refs_3_), channel_id=1, source_target_pairs={{0,4},{4,0},{8,12},{12,8},{1,5},{5,1},{9,13},{13,9},{2,6},{6,2},{1... | collective-permute-start | bytes 638984 | tf_op jit(solution)/shard_map/ppermute | solution.py:70
  41.1 4.3 %collective-permute-start.17 = (bf16[832,128]{1,0:T(8,128)(2,1)S(1)}, bf16[832,128]{1,0:T(8,128)(2,1)S(1)}, u32[]{:S(2)}, u32[]{:S(2)}) collective-permute-start(bf16[832,128]{1,0:T(8,128)(2,1)S(1)} %collective-permute-done.15.refs_0_), channel_id=1, source_target_pairs={{0,4},{4,0},{8,12},{12,8},{1,5},{5,1},{9,13},{13,9},{2,6},{6,2},{1... | collective-permute-start | bytes 638984 | tf_op jit(solution)/shard_map/ppermute | solution.py:70
  42.3 3.1 %collective-permute-start.18 = (bf16[832,128]{1,0:T(8,128)(2,1)S(1)}, bf16[832,128]{1,0:T(8,128)(2,1)S(1)}, u32[]{:S(2)}, u32[]{:S(2)}) collective-permute-start(bf16[832,128]{1,0:T(8,128)(2,1)S(1)} %collective-permute-done.16.refs_1_), channel_id=1, source_target_pairs={{0,4},{4,0},{8,12},{12,8},{1,5},{5,1},{9,13},{13,9},{2,6},{6,2},{1... | collective-permute-start | bytes 638984 | tf_op jit(solution)/shard_map/ppermute | solution.py:70
  44.7 2.1 %collective-permute-start.14 = (bf16[832,128]{1,0:T(8,128)(2,1)S(1)}, bf16[832,128]{1,0:T(8,128)(2,1)S(1)}, u32[]{:S(2)}, u32[]{:S(2)}) collective-permute-start(bf16[832,128]{1,0:T(8,128)(2,1)S(1)} %collective-permute-done.13.refs_2_), channel_id=1, source_target_pairs={{0,4},{4,0},{8,12},{12,8},{1,5},{5,1},{9,13},{13,9},{2,6},{6,2},{1... | collective-permute-start | bytes 638984 | tf_op jit(solution)/shard_map/ppermute | solution.py:70

commit v4 on v3

--- a/solution.py
+++ b/solution.py
@@ -74,9 +74,23 @@
     return tuple(a + b for a, b in zip(one, two))
 
 
-def dense_blocks(gradients, offsets, block, places, after):
+def dense_blocks(gradients, offsets, block, places, after, direct=False):
     rows = block // LANES
     total = len(offsets) * rows
+
+    def fetching(g_ref, keep_ref, send_ref, held, sems):
+        copies = []
+        for other in (True, False):
+            for offset in offsets:
+                start = pl.multiple_of(places.block(1, offset, other) * block, LANES)
+                at = len(copies)
+                copies.append(pltpu.make_async_copy(g_ref.at[:, pl.ds(start, block)], held.at[at], sems.at[at]))
+        for copy in copies:
+            copy.start()
+        for n, copy in enumerate(copies):
+            copy.wait()
+            out_ref, slot = (send_ref, keep_ref)[n // len(offsets)], n % len(offsets)
+            out_ref[slot * rows : (slot + 1) * rows, :] = held[n, 0, :].reshape(rows, LANES)
 
     def kernel(g_ref, *refs):
         keep_ref, send_ref = refs[len(after) :]
@@ -86,6 +100,21 @@
                 out_ref[slot * rows : (slot + 1) * rows, :] = g_ref[0, pl.ds(start, block)].reshape(rows, LANES)
 
     out = jax.ShapeDtypeStruct((total, LANES), gradients.dtype)
+    if direct:
+        return pl.pallas_call(
+            fetching,
+            in_specs=[pl.BlockSpec(memory_space=pltpu.HBM)],
+            out_specs=[pl.BlockSpec(memory_space=pltpu.VMEM)] * 2,
+            out_shape=[out, out],
+            scratch_shapes=[
+                pltpu.VMEM((2 * len(offsets), 1, block), gradients.dtype),
+                pltpu.SemaphoreType.DMA((2 * len(offsets),)),
+            ],
+            compiler_params=pltpu.CompilerParams(vmem_limit_bytes=VMEM_LIMIT),
+            cost_estimate=pl.CostEstimate(
+                flops=8 * total * LANES, bytes_accessed=12 * total * LANES, transcendentals=0
+            ),
+        )(pltpu.with_memory_space_constraint(gradients, pltpu.HBM))
     return pl.pallas_call(
         kernel,
         in_specs=[pl.BlockSpec(memory_space=pltpu.VMEM)] + [pl.BlockSpec(memory_space=pl.ANY)] * len(after),
@@ -145,8 +174,8 @@
     far = far[1:-1] + far[:1] + far[-1:]
     size = len(far) * rows
     values, after = {}, []
-    for part in (near[:1], near[2:3], near[1:2] + near[3:]):
-        keep, send = dense_blocks(gradients, [both(o, f) for o in part for f in far], owned, places, after)
+    for n, part in enumerate(filter(None, (near[:1], near[2:3], near[1:2] + near[3:]))):
+        keep, send = dense_blocks(gradients, [both(o, f) for o in part for f in far], owned, places, after, n == 0)
         after = [send]
         got = places.swap(send)
         for slot in range(len(part)):

time: 47.7 us -> 47.3 us (level)
  local copies, waits for them, and re-layouts: 2.01 us -> 0.32 us
  Pallas kernels: 2.35 us -> 3.76 us
  waiting for transfers between devices: 21.5 us -> 20.8 us
  starting transfers between devices: 18.1 us -> 18.7 us
    unnamed x8, local copies, waits for them, and re-layouts: 1.98 us -> 0.29 us
    pallas_call x0 -> x1, Pallas kernels: none -> 1.47 us  [dense_blocks(): pl.pallas_call(fetching, in_specs=[pl.BlockSpec(memory_space=pltpu.HBM)],...]
    ppermute x13, starting transfers between devices: 16.9 us -> 17.4 us  [send(): return lax.ppermute(value, ('gx', 'gy', 'gz'), moves)]
  transfers between devices with their start and end apart: 20 -> 20, of which waited for: 12 -> 11; matrix products, arithmetic and copies ran while one was open for 2% -> 2% of each run, Pallas kernels for 3% -> 3%
where the time goes in v4:
time: 47.3 us; the launch traced here: 47.1 us
  waiting for transfers between devices  20.8 us (44%)
  starting transfers between devices  18.7 us (40%)
  Pallas kernels  3.76 us (8%)
  between operations  2.28 us (5%)
  other arithmetic  1.31 us (3%)
    ppermute x13, waiting for transfers between devices, send(): return lax.ppermute(value, ('gx', 'gy', 'gz'), moves)  20.7 us
    ppermute x13, starting transfers between devices, send(): return lax.ppermute(value, ('gx', 'gy', 'gz'), moves)  17.4 us
    pallas_call x2, Pallas kernels, place_blocks(): pl.pallas_call(kernel, in_specs=[pl.BlockSpec(memory_space=pl.ANY)] * (le...  2.11 us
    pallas_call x1, Pallas kernels, dense_blocks(): pl.pallas_call(fetching, in_specs=[pl.BlockSpec(memory_space=pltpu.HBM)],...  1.47 us
    ppermute x7, starting transfers between devices, swap(): return lax.ppermute(value, 'gy', [(y, y ^ 1) for y in range(self.y)])  1.31 us
  transfers between devices with their start and end apart: 20, of which 11 were waited for; matrix products, arithmetic and copies ran while one was open for 2% of the time, Pallas kernels for 3%

profile of v4, /device:TPU:0, one launch (start us, length us, event | category | flops | bytes accessed | tf_op | source)
XLA Modules:
  0.0 47.1 jit_solution(10921645313127217606)
XLA Ops:
  0.6 1.5 %shard_map.93 = (bf16[832,128]{1,0:T(8,128)(2,1)S(1)}, bf16[832,128]{1,0:T(8,128)(2,1)S(1)}) custom-call(bf16[1,851968]{1,0:T(2,128)(2,1)} %g_ref.5), custom_call_target="tpu_custom_call" | custom-call | flops 851968 | bytes 1277952 | tf_op jit(solution)/shard_map/pallas_call | solution.py:104
  3.0 0.6 %collective-permute-start.1 = (bf16[832,128]{1,0:T(8,128)(2,1)S(1)}, bf16[832,128]{1,0:T(8,128)(2,1)S(1)}, u32[]{:S(2)}, u32[]{:S(2)}) collective-permute-start(bf16[832,128]{1,0:T(8,128)(2,1)S(1)} %get-tuple-element.22.refs_0_), channel_id=1, source_target_pairs={{0,4},{4,0},{8,12},{12,8},{1,5},{5,1},{9,13},{13,9},{2,6},{6,2},{1... | collective-permute-start | bytes 638984 | tf_op jit(solution)/shard_map/ppermute | solution.py:70
  3.9 3.0 %collective-permute-start.4 = (bf16[832,128]{1,0:T(8,128)(2,1)S(1)}, bf16[832,128]{1,0:T(8,128)(2,1)S(1)}, u32[]{:S(2)}, u32[]{:S(2)}) collective-permute-start(bf16[832,128]{1,0:T(8,128)(2,1)S(1)} %add_convert_fusion.1), channel_id=1, source_target_pairs={{0,16},{1,17},{2,18},{3,19},{4,12},{5,13},{6,14},{7,15},{8,24},{9,... | collective-permute-start | bytes 638984 | tf_op jit(solution)/shard_map/ppermute | solution.py:67
  7.0 0.7 %collective-permute-start.2 = (bf16[832,128]{1,0:T(8,128)(2,1)S(1)}, bf16[832,128]{1,0:T(8,128)(2,1)S(1)}, u32[]{:S(2)}, u32[]{:S(2)}) collective-permute-start(bf16[832,128]{1,0:T(8,128)(2,1)S(1)} %add_convert_fusion.2), channel_id=1, source_target_pairs={{0,16},{1,17},{2,18},{3,19},{4,12},{5,13},{6,14},{7,15},{8,24},{9,... | collective-permute-start | bytes 638984 | tf_op jit(solution)/shard_map/ppermute | solution.py:67
  7.7 3.1 %collective-permute-done.4 = bf16[832,128]{1,0:T(8,128)(2,1)S(1)} collective-permute-done((bf16[832,128]{1,0:T(8,128)(2,1)S(1)}, bf16[832,128]{1,0:T(8,128)(2,1)S(1)}, u32[]{:S(2)}, u32[]{:S(2)}) %collective-permute-start.4) | collective-permute-done | bytes 213024 | tf_op jit(solution)/shard_map/ppermute | solution.py:67
  10.9 2.1 %collective-permute-start.5 = (bf16[416,128]{1,0:T(8,128)(2,1)S(1)}, bf16[416,128]{1,0:T(8,128)(2,1)S(1)}, u32[]{:S(2)}, u32[]{:S(2)}) collective-permute-start(bf16[416,128]{1,0:T(8,128)(2,1)S(1)} %get-tuple-element.46), channel_id=1, source_target_pairs={{0,8},{1,9},{2,10},{3,11},{4,20},{5,21},{6,22},{7,23},{8,0},{9,1},... | collective-permute-start | bytes 319496 | tf_op jit(solution)/shard_map/ppermute | solution.py:67
  13.1 2.6 %collective-permute-done.5 = bf16[416,128]{1,0:T(8,128)(2,1)S(1)} collective-permute-done((bf16[416,128]{1,0:T(8,128)(2,1)S(1)}, bf16[416,128]{1,0:T(8,128)(2,1)S(1)}, u32[]{:S(2)}, u32[]{:S(2)}) %collective-permute-start.5) | collective-permute-done | bytes 106528 | tf_op jit(solution)/shard_map/ppermute | solution.py:67
  15.8 1.9 %collective-permute-done.6 = bf16[416,128]{1,0:T(8,128)(2,1)S(1)} collective-permute-done((bf16[416,128]{1,0:T(8,128)(2,1)S(1)}, bf16[416,128]{1,0:T(8,128)(2,1)S(1)}, u32[]{:S(2)}, u32[]{:S(2)}) %collective-permute-start.6) | collective-permute-done | bytes 106528 | tf_op jit(solution)/shard_map/ppermute | solution.py:67
  17.7 1.6 %collective-permute-start.9 = (bf16[208,128]{1,0:T(8,128)(2,1)S(1)}, bf16[208,128]{1,0:T(8,128)(2,1)S(1)}, u32[]{:S(2)}, u32[]{:S(2)}) collective-permute-start(bf16[208,128]{1,0:T(8,128)(2,1)S(1)} %slice.78), channel_id=1, source_target_pairs={{0,1},{1,0},{2,3},{3,2},{4,5},{5,4},{6,7},{7,6},{8,9},{9,8},{10,11... | collective-permute-start | bytes 159752 | tf_op jit(solution)/shard_map/ppermute | solution.py:67
  19.3 2.6 %collective-permute-start.7 = (bf16[208,128]{1,0:T(8,128)(2,1)S(1)}, bf16[208,128]{1,0:T(8,128)(2,1)S(1)}, u32[]{:S(2)}, u32[]{:S(2)}) collective-permute-start(bf16[208,128]{1,0:T(8,128)(2,1)S(1)} %get-tuple-element.48), channel_id=1, source_target_pairs={{0,2},{1,3},{2,0},{3,1},{4,6},{5,7},{6,4},{7,5},{8,10},{9,11},{10,... | collective-permute-start | bytes 159752 | tf_op jit(solution)/shard_map/ppermute | solution.py:67
  23.6 2.0 %collective-permute-done.7 = bf16[208,128]{1,0:T(8,128)(2,1)S(1)} collective-permute-done((bf16[208,128]{1,0:T(8,128)(2,1)S(1)}, bf16[208,128]{1,0:T(8,128)(2,1)S(1)}, u32[]{:S(2)}, u32[]{:S(2)}) %collective-permute-start.7) | collective-permute-done | bytes 53280 | tf_op jit(solution)/shard_map/ppermute | solution.py:67
  25.5 2.6 %collective-permute-done.8 = bf16[208,128]{1,0:T(8,128)(2,1)S(1)} collective-permute-done((bf16[208,128]{1,0:T(8,128)(2,1)S(1)}, bf16[208,128]{1,0:T(8,128)(2,1)S(1)}, u32[]{:S(2)}, u32[]{:S(2)}) %collective-permute-start.8) | collective-permute-done | bytes 53280 | tf_op jit(solution)/shard_map/ppermute | solution.py:67
  28.3 0.9 %collective-permute-start.11 = (bf16[208,128]{1,0:T(8,128)(2,1)S(1)}, bf16[208,128]{1,0:T(8,128)(2,1)S(1)}, u32[]{:S(2)}, u32[]{:S(2)}) collective-permute-start(bf16[208,128]{1,0:T(8,128)(2,1)S(1)} %get-tuple-element.38), channel_id=1, source_target_pairs={{0,3},{1,2},{2,1},{3,0},{4,7},{5,6},{6,5},{7,4},{8,11},{9,10},{10,... | collective-permute-start | bytes 159752 | tf_op jit(solution)/shard_map/ppermute | solution.py:67
  29.2 2.6 %collective-permute-start.12 = (bf16[208,128]{1,0:T(8,128)(2,1)S(1)}, bf16[208,128]{1,0:T(8,128)(2,1)S(1)}, u32[]{:S(2)}, u32[]{:S(2)}) collective-permute-start(bf16[208,128]{1,0:T(8,128)(2,1)S(1)} %get-tuple-element.38), channel_id=1, source_target_pairs={{0,1},{1,0},{2,3},{3,2},{4,5},{5,4},{6,7},{7,6},{8,9},{9,8},{10,11... | collective-permute-start | bytes 159752 | tf_op jit(solution)/shard_map/ppermute | solution.py:67
  31.8 1.5 %collective-permute-done.10 = bf16[208,128]{1,0:T(8,128)(2,1)S(1)} collective-permute-done((bf16[208,128]{1,0:T(8,128)(2,1)S(1)}, bf16[208,128]{1,0:T(8,128)(2,1)S(1)}, u32[]{:S(2)}, u32[]{:S(2)}) %collective-permute-start.10) | collective-permute-done | bytes 53280 | tf_op jit(solution)/shard_map/ppermute | solution.py:67
  33.3 1.1 %collective-permute-done.11 = bf16[208,128]{1,0:T(8,128)(2,1)S(1)} collective-permute-done((bf16[208,128]{1,0:T(8,128)(2,1)S(1)}, bf16[208,128]{1,0:T(8,128)(2,1)S(1)}, u32[]{:S(2)}, u32[]{:S(2)}) %collective-permute-start.11) | collective-permute-done | bytes 53280 | tf_op jit(solution)/shard_map/ppermute | solution.py:67
  34.5 1.6 %collective-permute-start.15 = (bf16[832,128]{1,0:T(8,128)(2,1)S(1)}, bf16[832,128]{1,0:T(8,128)(2,1)S(1)}, u32[]{:S(2)}, u32[]{:S(2)}) collective-permute-start(bf16[832,128]{1,0:T(8,128)(2,1)S(1)} %pad_maximum_fusion.refs_3_), channel_id=1, source_target_pairs={{0,16},{1,17},{2,18},{3,19},{4,12},{5,13},{6,14},{7,15},{8,24},{9,... | collective-permute-start | bytes 638984 | tf_op jit(solution)/shard_map/ppermute | solution.py:67
  36.1 1.4 %collective-permute-start.16 = (bf16[832,128]{1,0:T(8,128)(2,1)S(1)}, bf16[832,128]{1,0:T(8,128)(2,1)S(1)}, u32[]{:S(2)}, u32[]{:S(2)}) collective-permute-start(bf16[832,128]{1,0:T(8,128)(2,1)S(1)} %pad_maximum_fusion.refs_3_), channel_id=1, source_target_pairs={{0,8},{1,9},{2,10},{3,11},{4,20},{5,21},{6,22},{7,23},{8,0},{9,1},... | collective-permute-start | bytes 638984 | tf_op jit(solution)/shard_map/ppermute | solution.py:67
  38.2 2.5 %collective-permute-done.15.refs_0_ = bf16[832,128]{1,0:T(8,128)(2,1)S(1)} collective-permute-done((bf16[832,128]{1,0:T(8,128)(2,1)S(1)}, bf16[832,128]{1,0:T(8,128)(2,1)S(1)}, u32[]{:S(2)}, u32[]{:S(2)}) %collective-permute-start.15) | collective-permute-done | bytes 213024 | tf_op jit(solution)/shard_map/ppermute | solution.py:67
  40.7 1.2 %collective-permute-done.16.refs_1_ = bf16[832,128]{1,0:T(8,128)(2,1)S(1)} collective-permute-done((bf16[832,128]{1,0:T(8,128)(2,1)S(1)}, bf16[832,128]{1,0:T(8,128)(2,1)S(1)}, u32[]{:S(2)}, u32[]{:S(2)}) %collective-permute-start.16) | collective-permute-done | bytes 213024 | tf_op jit(solution)/shard_map/ppermute | solution.py:67
  41.9 2.3 %collective-permute-done.13.refs_2_ = bf16[832,128]{1,0:T(8,128)(2,1)S(1)} collective-permute-done((bf16[832,128]{1,0:T(8,128)(2,1)S(1)}, bf16[832,128]{1,0:T(8,128)(2,1)S(1)}, u32[]{:S(2)}, u32[]{:S(2)}) %collective-permute-start.13) | collective-permute-done | bytes 213024 | tf_op jit(solution)/shard_map/ppermute | solution.py:67
  44.3 0.7 %multiply_subtract_fusion = (f32[26624]{0:T(1024)}, f32[26624]{0:T(1024)}, f32[26624]{0:T(1024)}) fusion(f32[26624]{0:T(1024)S(1)} %copy-done.1, f32[]{:T(128)} %bitcast.3, f32[]{:T(128)} %bitcast.2, f32[]{:T(128)} %bitcast.12, f32[26624]{0:T(1024)S(1)} %get-tuple-element.35, f32[26624]{0:T(1024)S(1)} %copy-done.2, f32[26624]{0:T(1024)S(1)} %copy-done.3), kind=kLoop, calls=%fused_computation.23 | loop fusion | flops 346112 | bytes 745484 | tf_op jit(solution)/shard_map/sub | solution.py:26
  45.0 1.4 %shard_map.96.refs_1_ = bf16[6656,128]{1,0:T(8,128)(2,1)} custom-call(bf16[832,128]{1,0:T(8,128)(2,1)S(1)} %collective-permute-done.15.refs_0_, bf16[832,128]{1,0:T(8,128)(2,1)S(1)} %collective-permute-done.16.refs_1_, bf16[832,128]{1,0:T(8,128)(2,1)S(1)} %collective-permute-done.13.refs_2_, bf16[832,128]{1,0:T(8,128)(2,1)S(1)} %pad_maximum_fusion.refs_3_, ...), custom_call_target="tpu_custom_call" | custom-call | flops 851968 | bytes 3407872 | tf_op jit(solution)/shard_map/pallas_call | solution.py:154
  46.4 0.7 %shard_map.97 = bf16[6656,128]{1,0:T(8,128)(2,1)} custom-call(bf16[832,128]{1,0:T(8,128)(2,1)S(1)} %collective-permute-done.14.refs_0_, bf16[6656,128]{1,0:T(8,128)(2,1)} %shard_map.96.refs_1_), custom_call_target="tpu_custom_call", output_to_operand_aliasing={{}: (1, {})} | custom-call | flops 851968 | bytes 3407872 | tf_op jit(solution)/shard_map/pallas_call | solution.py:154
  (44 shorter events, 2.8 us)
Async XLA Ops:
  0.6 2.3 %copy-start = (bf16[1,851968]{1,0:T(2,128)(2,1)S(1)}, bf16[1,851968]{1,0:T(2,128)(2,1)}, u32[]{:S(2)}) copy-start(bf16[1,851968]{1,0:T(2,128)(2,1)} %g_ref.5) | copy-start | bytes 5111812
  2.1 1.7 %collective-permute-start.3 = (bf16[832,128]{1,0:T(8,128)(2,1)S(1)}, bf16[832,128]{1,0:T(8,128)(2,1)S(1)}, u32[]{:S(2)}, u32[]{:S(2)}) collective-permute-start(bf16[832,128]{1,0:T(8,128)(2,1)S(1)} %get-tuple-element.21.refs_0_), channel_id=1, source_target_pairs={{0,4},{4,0},{8,12},{12,8},{1,5},{5,1},{9,13},{13,9},{2,6},{6,2},{1... | collective-permute-start | bytes 638984 | tf_op jit(solution)/shard_map/ppermute | solution.py:70
  3.0 3.9 %collective-permute-start.1 = (bf16[832,128]{1,0:T(8,128)(2,1)S(1)}, bf16[832,128]{1,0:T(8,128)(2,1)S(1)}, u32[]{:S(2)}, u32[]{:S(2)}) collective-permute-start(bf16[832,128]{1,0:T(8,128)(2,1)S(1)} %get-tuple-element.22.refs_0_), channel_id=1, source_target_pairs={{0,4},{4,0},{8,12},{12,8},{1,5},{5,1},{9,13},{13,9},{2,6},{6,2},{1... | collective-permute-start | bytes 638984 | tf_op jit(solution)/shard_map/ppermute | solution.py:70
  3.7 4.0 %collective-permute-start = (bf16[1664,128]{1,0:T(8,128)(2,1)S(1)}, bf16[1664,128]{1,0:T(8,128)(2,1)S(1)}, u32[]{:S(2)}, u32[]{:S(2)}) collective-permute-start(bf16[1664,128]{1,0:T(8,128)(2,1)S(1)} %get-tuple-element.24), channel_id=1, source_target_pairs={{0,4},{4,0},{8,12},{12,8},{1,5},{5,1},{9,13},{13,9},{2,6},{6,2},{1... | collective-permute-start | bytes 1277960 | tf_op jit(solution)/shard_map/ppermute | solution.py:70
  3.9 6.9 %collective-permute-start.4 = (bf16[832,128]{1,0:T(8,128)(2,1)S(1)}, bf16[832,128]{1,0:T(8,128)(2,1)S(1)}, u32[]{:S(2)}, u32[]{:S(2)}) collective-permute-start(bf16[832,128]{1,0:T(8,128)(2,1)S(1)} %add_convert_fusion.1), channel_id=1, source_target_pairs={{0,16},{1,17},{2,18},{3,19},{4,12},{5,13},{6,14},{7,15},{8,24},{9,... | collective-permute-start | bytes 638984 | tf_op jit(solution)/shard_map/ppermute | solution.py:67
  7.0 6.1 %collective-permute-start.2 = (bf16[832,128]{1,0:T(8,128)(2,1)S(1)}, bf16[832,128]{1,0:T(8,128)(2,1)S(1)}, u32[]{:S(2)}, u32[]{:S(2)}) collective-permute-start(bf16[832,128]{1,0:T(8,128)(2,1)S(1)} %add_convert_fusion.2), channel_id=1, source_target_pairs={{0,16},{1,17},{2,18},{3,19},{4,12},{5,13},{6,14},{7,15},{8,24},{9,... | collective-permute-start | bytes 638984 | tf_op jit(solution)/shard_map/ppermute | solution.py:67
  10.9 4.8 %collective-permute-start.5 = (bf16[416,128]{1,0:T(8,128)(2,1)S(1)}, bf16[416,128]{1,0:T(8,128)(2,1)S(1)}, u32[]{:S(2)}, u32[]{:S(2)}) collective-permute-start(bf16[416,128]{1,0:T(8,128)(2,1)S(1)} %get-tuple-element.46), channel_id=1, source_target_pairs={{0,8},{1,9},{2,10},{3,11},{4,20},{5,21},{6,22},{7,23},{8,0},{9,1},... | collective-permute-start | bytes 319496 | tf_op jit(solution)/shard_map/ppermute | solution.py:67
  12.9 4.7 %collective-permute-start.6 = (bf16[416,128]{1,0:T(8,128)(2,1)S(1)}, bf16[416,128]{1,0:T(8,128)(2,1)S(1)}, u32[]{:S(2)}, u32[]{:S(2)}) collective-permute-start(bf16[416,128]{1,0:T(8,128)(2,1)S(1)} %get-tuple-element.45), channel_id=1, source_target_pairs={{0,8},{1,9},{2,10},{3,11},{4,20},{5,21},{6,22},{7,23},{8,0},{9,1},... | collective-permute-start | bytes 319496 | tf_op jit(solution)/shard_map/ppermute | solution.py:67
  13.0 15.0 %copy-start.1 = (f32[26624]{0:T(1024)S(1)}, f32[26624]{0:T(1024)}, u32[]{:S(2)}) copy-start(f32[26624]{0:T(1024)} %param.7) | copy-start | bytes 319492
  13.1 15.0 %copy-start.2 = (f32[26624]{0:T(1024)S(1)}, f32[26624]{0:T(1024)}, u32[]{:S(2)}) copy-start(f32[26624]{0:T(1024)} %param.9) | copy-start | bytes 319492
  13.1 15.0 %copy-start.3 = (f32[26624]{0:T(1024)S(1)}, f32[26624]{0:T(1024)}, u32[]{:S(2)}) copy-start(f32[26624]{0:T(1024)} %param.8) | copy-start | bytes 319492
  17.7 5.8 %collective-permute-start.9 = (bf16[208,128]{1,0:T(8,128)(2,1)S(1)}, bf16[208,128]{1,0:T(8,128)(2,1)S(1)}, u32[]{:S(2)}, u32[]{:S(2)}) collective-permute-start(bf16[208,128]{1,0:T(8,128)(2,1)S(1)} %slice.78), channel_id=1, source_target_pairs={{0,1},{1,0},{2,3},{3,2},{4,5},{5,4},{6,7},{7,6},{8,9},{9,8},{10,11... | collective-permute-start | bytes 159752 | tf_op jit(solution)/shard_map/ppermute | solution.py:67
  19.3 6.2 %collective-permute-start.7 = (bf16[208,128]{1,0:T(8,128)(2,1)S(1)}, bf16[208,128]{1,0:T(8,128)(2,1)S(1)}, u32[]{:S(2)}, u32[]{:S(2)}) collective-permute-start(bf16[208,128]{1,0:T(8,128)(2,1)S(1)} %get-tuple-element.48), channel_id=1, source_target_pairs={{0,2},{1,3},{2,0},{3,1},{4,6},{5,7},{6,4},{7,5},{8,10},{9,11},{10,... | collective-permute-start | bytes 159752 | tf_op jit(solution)/shard_map/ppermute | solution.py:67
  21.9 6.2 %collective-permute-start.8 = (bf16[208,128]{1,0:T(8,128)(2,1)S(1)}, bf16[208,128]{1,0:T(8,128)(2,1)S(1)}, u32[]{:S(2)}, u32[]{:S(2)}) collective-permute-start(bf16[208,128]{1,0:T(8,128)(2,1)S(1)} %get-tuple-element.47), channel_id=1, source_target_pairs={{0,3},{1,2},{2,1},{3,0},{4,7},{5,6},{6,5},{7,4},{8,11},{9,10},{10,... | collective-permute-start | bytes 159752 | tf_op jit(solution)/shard_map/ppermute | solution.py:67
  28.2 5.1 %collective-permute-start.10 = (bf16[208,128]{1,0:T(8,128)(2,1)S(1)}, bf16[208,128]{1,0:T(8,128)(2,1)S(1)}, u32[]{:S(2)}, u32[]{:S(2)}) collective-permute-start(bf16[208,128]{1,0:T(8,128)(2,1)S(1)} %get-tuple-element.38), channel_id=1, source_target_pairs={{0,2},{1,3},{2,0},{3,1},{4,6},{5,7},{6,4},{7,5},{8,10},{9,11},{10,... | collective-permute-start | bytes 159752 | tf_op jit(solution)/shard_map/ppermute | solution.py:67
  28.3 6.1 %collective-permute-start.11 = (bf16[208,128]{1,0:T(8,128)(2,1)S(1)}, bf16[208,128]{1,0:T(8,128)(2,1)S(1)}, u32[]{:S(2)}, u32[]{:S(2)}) collective-permute-start(bf16[208,128]{1,0:T(8,128)(2,1)S(1)} %get-tuple-element.38), channel_id=1, source_target_pairs={{0,3},{1,2},{2,1},{3,0},{4,7},{5,6},{6,5},{7,4},{8,11},{9,10},{10,... | collective-permute-start | bytes 159752 | tf_op jit(solution)/shard_map/ppermute | solution.py:67
  29.2 5.2 %collective-permute-start.12 = (bf16[208,128]{1,0:T(8,128)(2,1)S(1)}, bf16[208,128]{1,0:T(8,128)(2,1)S(1)}, u32[]{:S(2)}, u32[]{:S(2)}) collective-permute-start(bf16[208,128]{1,0:T(8,128)(2,1)S(1)} %get-tuple-element.38), channel_id=1, source_target_pairs={{0,1},{1,0},{2,3},{3,2},{4,5},{5,4},{6,7},{7,6},{8,9},{9,8},{10,11... | collective-permute-start | bytes 159752 | tf_op jit(solution)/shard_map/ppermute | solution.py:67
  34.5 6.2 %collective-permute-start.15 = (bf16[832,128]{1,0:T(8,128)(2,1)S(1)}, bf16[832,128]{1,0:T(8,128)(2,1)S(1)}, u32[]{:S(2)}, u32[]{:S(2)}) collective-permute-start(bf16[832,128]{1,0:T(8,128)(2,1)S(1)} %pad_maximum_fusion.refs_3_), channel_id=1, source_target_pairs={{0,16},{1,17},{2,18},{3,19},{4,12},{5,13},{6,14},{7,15},{8,24},{9,... | collective-permute-start | bytes 638984 | tf_op jit(solution)/shard_map/ppermute | solution.py:67
  36.1 5.8 %collective-permute-start.16 = (bf16[832,128]{1,0:T(8,128)(2,1)S(1)}, bf16[832,128]{1,0:T(8,128)(2,1)S(1)}, u32[]{:S(2)}, u32[]{:S(2)}) collective-permute-start(bf16[832,128]{1,0:T(8,128)(2,1)S(1)} %pad_maximum_fusion.refs_3_), channel_id=1, source_target_pairs={{0,8},{1,9},{2,10},{3,11},{4,20},{5,21},{6,22},{7,23},{8,0},{9,1},... | collective-permute-start | bytes 638984 | tf_op jit(solution)/shard_map/ppermute | solution.py:67
  37.5 6.7 %collective-permute-start.13 = (bf16[832,128]{1,0:T(8,128)(2,1)S(1)}, bf16[832,128]{1,0:T(8,128)(2,1)S(1)}, u32[]{:S(2)}, u32[]{:S(2)}) collective-permute-start(bf16[832,128]{1,0:T(8,128)(2,1)S(1)} %pad_maximum_fusion.refs_3_), channel_id=1, source_target_pairs={{0,24},{1,25},{2,26},{3,27},{4,28},{5,29},{6,30},{7,31},{8,16},{9,... | collective-permute-start | bytes 638984 | tf_op jit(solution)/shard_map/ppermute | solution.py:67
  38.1 6.9 %collective-permute-start.19 = (bf16[832,128]{1,0:T(8,128)(2,1)S(1)}, bf16[832,128]{1,0:T(8,128)(2,1)S(1)}, u32[]{:S(2)}, u32[]{:S(2)}) collective-permute-start(bf16[832,128]{1,0:T(8,128)(2,1)S(1)} %pad_maximum_fusion.refs_3_), channel_id=1, source_target_pairs={{0,4},{4,0},{8,12},{12,8},{1,5},{5,1},{9,13},{13,9},{2,6},{6,2},{1... | collective-permute-start | bytes 638984 | tf_op jit(solution)/shard_map/ppermute | solution.py:70
  40.7 4.3 %collective-permute-start.17 = (bf16[832,128]{1,0:T(8,128)(2,1)S(1)}, bf16[832,128]{1,0:T(8,128)(2,1)S(1)}, u32[]{:S(2)}, u32[]{:S(2)}) collective-permute-start(bf16[832,128]{1,0:T(8,128)(2,1)S(1)} %collective-permute-done.15.refs_0_), channel_id=1, source_target_pairs={{0,4},{4,0},{8,12},{12,8},{1,5},{5,1},{9,13},{13,9},{2,6},{6,2},{1... | collective-permute-start | bytes 638984 | tf_op jit(solution)/shard_map/ppermute | solution.py:70
  41.9 3.1 %collective-permute-start.18 = (bf16[832,128]{1,0:T(8,128)(2,1)S(1)}, bf16[832,128]{1,0:T(8,128)(2,1)S(1)}, u32[]{:S(2)}, u32[]{:S(2)}) collective-permute-start(bf16[832,128]{1,0:T(8,128)(2,1)S(1)} %collective-permute-done.16.refs_1_), channel_id=1, source_target_pairs={{0,4},{4,0},{8,12},{12,8},{1,5},{5,1},{9,13},{13,9},{2,6},{6,2},{1... | collective-permute-start | bytes 638984 | tf_op jit(solution)/shard_map/ppermute | solution.py:70
  44.3 2.1 %collective-permute-start.14 = (bf16[832,128]{1,0:T(8,128)(2,1)S(1)}, bf16[832,128]{1,0:T(8,128)(2,1)S(1)}, u32[]{:S(2)}, u32[]{:S(2)}) collective-permute-start(bf16[832,128]{1,0:T(8,128)(2,1)S(1)} %collective-permute-done.13.refs_2_), channel_id=1, source_target_pairs={{0,4},{4,0},{8,12},{12,8},{1,5},{5,1},{9,13},{13,9},{2,6},{6,2},{1... | collective-permute-start | bytes 638984 | tf_op jit(solution)/shard_map/ppermute | solution.py:70

commit v5 on v4

--- a/solution.py
+++ b/solution.py
@@ -78,53 +78,53 @@
     rows = block // LANES
     total = len(offsets) * rows
 
-    def fetching(g_ref, keep_ref, send_ref, held, sems):
+    def fetching(g_ref, send_ref, held, sems):
         copies = []
-        for other in (True, False):
-            for offset in offsets:
-                start = pl.multiple_of(places.block(1, offset, other) * block, LANES)
-                at = len(copies)
-                copies.append(pltpu.make_async_copy(g_ref.at[:, pl.ds(start, block)], held.at[at], sems.at[at]))
+        for at, offset in enumerate(offsets):
+            start = pl.multiple_of(places.block(1, offset, True) * block, LANES)
+            copies.append(pltpu.make_async_copy(g_ref.at[:, pl.ds(start, block)], held.at[at], sems.at[at]))
         for copy in copies:
             copy.start()
         for n, copy in enumerate(copies):
             copy.wait()
-            out_ref, slot = (send_ref, keep_ref)[n // len(offsets)], n % len(offsets)
-            out_ref[slot * rows : (slot + 1) * rows, :] = held[n, 0, :].reshape(rows, LANES)
+            send_ref[n * rows : (n + 1) * rows, :] = held[n, 0, :].reshape(rows, LANES)
 
     def kernel(g_ref, *refs):
-        keep_ref, send_ref = refs[len(after) :]
-        for other, out_ref in ((True, send_ref), (False, keep_ref)):
+        outs = refs[len(after) :]
+        for other, out_ref in zip((False, True), outs):
             for slot, offset in enumerate(offsets):
                 start = pl.multiple_of(places.block(1, offset, other) * block, LANES)
                 out_ref[slot * rows : (slot + 1) * rows, :] = g_ref[0, pl.ds(start, block)].reshape(rows, LANES)
 
     out = jax.ShapeDtypeStruct((total, LANES), gradients.dtype)
     if direct:
-        return pl.pallas_call(
+        send = pl.pallas_call(
             fetching,
             in_specs=[pl.BlockSpec(memory_space=pltpu.HBM)],
-            out_specs=[pl.BlockSpec(memory_space=pltpu.VMEM)] * 2,
-            out_shape=[out, out],
+            out_specs=pl.BlockSpec(memory_space=pltpu.VMEM),
+            out_shape=out,
             scratch_shapes=[
-                pltpu.VMEM((2 * len(offsets), 1, block), gradients.dtype),
-                pltpu.SemaphoreType.DMA((2 * len(offsets),)),
+                pltpu.VMEM((len(offsets), 1, block), gradients.dtype),
+                pltpu.SemaphoreType.DMA((len(offsets),)),
             ],
             compiler_params=pltpu.CompilerParams(vmem_limit_bytes=VMEM_LIMIT),
             cost_estimate=pl.CostEstimate(
-                flops=8 * total * LANES, bytes_accessed=12 * total * LANES, transcendentals=0
+                flops=4 * total * LANES, bytes_accessed=6 * total * LANES, transcendentals=0
             ),
         )(pltpu.with_memory_space_constraint(gradients, pltpu.HBM))
-    return pl.pallas_call(
+        after = [send]
+    sides = 1 if direct else 2
+    made = pl.pallas_call(
         kernel,
         in_specs=[pl.BlockSpec(memory_space=pltpu.VMEM)] + [pl.BlockSpec(memory_space=pl.ANY)] * len(after),
-        out_specs=[pl.BlockSpec(memory_space=pltpu.VMEM)] * 2,
-        out_shape=[out, out],
+        out_specs=[pl.BlockSpec(memory_space=pltpu.VMEM)] * sides,
+        out_shape=[out] * sides,
         compiler_params=pltpu.CompilerParams(vmem_limit_bytes=VMEM_LIMIT),
         cost_estimate=pl.CostEstimate(
             flops=8 * total * LANES, bytes_accessed=12 * total * LANES, transcendentals=0
         ),
     )(gradients, *after)
+    return (*made, send) if direct else made
 
 
 def place_blocks(pieces, held, block, total, places, into=()):

time: 47.3 us -> 47.2 us (level)
  no operation moved by 1% of the time
where the time goes in v5:
time: 47.2 us; the launch traced here: 47 us
  waiting for transfers between devices  20.8 us (44%)
  starting transfers between devices  18.7 us (40%)
  Pallas kernels  3.59 us (8%)
  between operations  2.3 us (5%)
  other arithmetic  1.31 us (3%)
    ppermute x13, waiting for transfers between devices, send(): return lax.ppermute(value, ('gx', 'gy', 'gz'), moves)  20.8 us
    ppermute x13, starting transfers between devices, send(): return lax.ppermute(value, ('gx', 'gy', 'gz'), moves)  17.4 us
    pallas_call x2, Pallas kernels, place_blocks(): pl.pallas_call(kernel, in_specs=[pl.BlockSpec(memory_space=pl.ANY)] * (le...  2.11 us
    ppermute x7, starting transfers between devices, swap(): return lax.ppermute(value, 'gy', [(y, y ^ 1) for y in range(self.y)])  1.31 us
    pallas_call x1, Pallas kernels, dense_blocks(): pl.pallas_call(fetching, in_specs=[pl.BlockSpec(memory_space=pltpu.HBM)],...  1.27 us
  transfers between devices with their start and end apart: 20, of which 11 were waited for; matrix products, arithmetic and copies ran while one was open for 2% of the time, Pallas kernels for 3%

profile of v5, /device:TPU:0, one launch (start us, length us, event | category | flops | bytes accessed | tf_op | source)
XLA Modules:
  0.0 47.0 jit_solution(523507777397460682)
XLA Ops:
  0.6 1.3 %shard_map.93.refs_0_ = bf16[832,128]{1,0:T(8,128)(2,1)S(1)} custom-call(bf16[1,851968]{1,0:T(2,128)(2,1)} %g_ref.7), custom_call_target="tpu_custom_call" | custom-call | flops 425984 | bytes 638976 | tf_op jit(solution)/shard_map/pallas_call | solution.py:101
  2.9 0.6 %collective-permute-start.1 = (bf16[832,128]{1,0:T(8,128)(2,1)S(1)}, bf16[832,128]{1,0:T(8,128)(2,1)S(1)}, u32[]{:S(2)}, u32[]{:S(2)}) collective-permute-start(bf16[832,128]{1,0:T(8,128)(2,1)S(1)} %get-tuple-element.19.refs_0_), channel_id=1, source_target_pairs={{0,4},{4,0},{8,12},{12,8},{1,5},{5,1},{9,13},{13,9},{2,6},{6,2},{1... | collective-permute-start | bytes 638984 | tf_op jit(solution)/shard_map/ppermute | solution.py:70
  3.8 3.0 %collective-permute-start.4 = (bf16[832,128]{1,0:T(8,128)(2,1)S(1)}, bf16[832,128]{1,0:T(8,128)(2,1)S(1)}, u32[]{:S(2)}, u32[]{:S(2)}) collective-permute-start(bf16[832,128]{1,0:T(8,128)(2,1)S(1)} %add_convert_fusion.1), channel_id=1, source_target_pairs={{0,16},{1,17},{2,18},{3,19},{4,12},{5,13},{6,14},{7,15},{8,24},{9,... | collective-permute-start | bytes 638984 | tf_op jit(solution)/shard_map/ppermute | solution.py:67
  6.9 0.7 %collective-permute-start.2 = (bf16[832,128]{1,0:T(8,128)(2,1)S(1)}, bf16[832,128]{1,0:T(8,128)(2,1)S(1)}, u32[]{:S(2)}, u32[]{:S(2)}) collective-permute-start(bf16[832,128]{1,0:T(8,128)(2,1)S(1)} %add_convert_fusion.2), channel_id=1, source_target_pairs={{0,16},{1,17},{2,18},{3,19},{4,12},{5,13},{6,14},{7,15},{8,24},{9,... | collective-permute-start | bytes 638984 | tf_op jit(solution)/shard_map/ppermute | solution.py:67
  7.5 3.1 %collective-permute-done.4 = bf16[832,128]{1,0:T(8,128)(2,1)S(1)} collective-permute-done((bf16[832,128]{1,0:T(8,128)(2,1)S(1)}, bf16[832,128]{1,0:T(8,128)(2,1)S(1)}, u32[]{:S(2)}, u32[]{:S(2)}) %collective-permute-start.4) | collective-permute-done | bytes 213024 | tf_op jit(solution)/shard_map/ppermute | solution.py:67
  10.8 2.1 %collective-permute-start.5 = (bf16[416,128]{1,0:T(8,128)(2,1)S(1)}, bf16[416,128]{1,0:T(8,128)(2,1)S(1)}, u32[]{:S(2)}, u32[]{:S(2)}) collective-permute-start(bf16[416,128]{1,0:T(8,128)(2,1)S(1)} %get-tuple-element.42), channel_id=1, source_target_pairs={{0,8},{1,9},{2,10},{3,11},{4,20},{5,21},{6,22},{7,23},{8,0},{9,1},... | collective-permute-start | bytes 319496 | tf_op jit(solution)/shard_map/ppermute | solution.py:67
  13.0 2.6 %collective-permute-done.5 = bf16[416,128]{1,0:T(8,128)(2,1)S(1)} collective-permute-done((bf16[416,128]{1,0:T(8,128)(2,1)S(1)}, bf16[416,128]{1,0:T(8,128)(2,1)S(1)}, u32[]{:S(2)}, u32[]{:S(2)}) %collective-permute-start.5) | collective-permute-done | bytes 106528 | tf_op jit(solution)/shard_map/ppermute | solution.py:67
  15.7 1.9 %collective-permute-done.6 = bf16[416,128]{1,0:T(8,128)(2,1)S(1)} collective-permute-done((bf16[416,128]{1,0:T(8,128)(2,1)S(1)}, bf16[416,128]{1,0:T(8,128)(2,1)S(1)}, u32[]{:S(2)}, u32[]{:S(2)}) %collective-permute-start.6) | collective-permute-done | bytes 106528 | tf_op jit(solution)/shard_map/ppermute | solution.py:67
  17.6 1.6 %collective-permute-start.9 = (bf16[208,128]{1,0:T(8,128)(2,1)S(1)}, bf16[208,128]{1,0:T(8,128)(2,1)S(1)}, u32[]{:S(2)}, u32[]{:S(2)}) collective-permute-start(bf16[208,128]{1,0:T(8,128)(2,1)S(1)} %slice.78), channel_id=1, source_target_pairs={{0,1},{1,0},{2,3},{3,2},{4,5},{5,4},{6,7},{7,6},{8,9},{9,8},{10,11... | collective-permute-start | bytes 159752 | tf_op jit(solution)/shard_map/ppermute | solution.py:67
  19.2 2.6 %collective-permute-start.7 = (bf16[208,128]{1,0:T(8,128)(2,1)S(1)}, bf16[208,128]{1,0:T(8,128)(2,1)S(1)}, u32[]{:S(2)}, u32[]{:S(2)}) collective-permute-start(bf16[208,128]{1,0:T(8,128)(2,1)S(1)} %get-tuple-element.44), channel_id=1, source_target_pairs={{0,2},{1,3},{2,0},{3,1},{4,6},{5,7},{6,4},{7,5},{8,10},{9,11},{10,... | collective-permute-start | bytes 159752 | tf_op jit(solution)/shard_map/ppermute | solution.py:67
  23.5 2.0 %collective-permute-done.7 = bf16[208,128]{1,0:T(8,128)(2,1)S(1)} collective-permute-done((bf16[208,128]{1,0:T(8,128)(2,1)S(1)}, bf16[208,128]{1,0:T(8,128)(2,1)S(1)}, u32[]{:S(2)}, u32[]{:S(2)}) %collective-permute-start.7) | collective-permute-done | bytes 53280 | tf_op jit(solution)/shard_map/ppermute | solution.py:67
  25.4 2.6 %collective-permute-done.8 = bf16[208,128]{1,0:T(8,128)(2,1)S(1)} collective-permute-done((bf16[208,128]{1,0:T(8,128)(2,1)S(1)}, bf16[208,128]{1,0:T(8,128)(2,1)S(1)}, u32[]{:S(2)}, u32[]{:S(2)}) %collective-permute-start.8) | collective-permute-done | bytes 53280 | tf_op jit(solution)/shard_map/ppermute | solution.py:67
  28.2 0.9 %collective-permute-start.11 = (bf16[208,128]{1,0:T(8,128)(2,1)S(1)}, bf16[208,128]{1,0:T(8,128)(2,1)S(1)}, u32[]{:S(2)}, u32[]{:S(2)}) collective-permute-start(bf16[208,128]{1,0:T(8,128)(2,1)S(1)} %get-tuple-element.34), channel_id=1, source_target_pairs={{0,3},{1,2},{2,1},{3,0},{4,7},{5,6},{6,5},{7,4},{8,11},{9,10},{10,... | collective-permute-start | bytes 159752 | tf_op jit(solution)/shard_map/ppermute | solution.py:67
  29.1 2.6 %collective-permute-start.12 = (bf16[208,128]{1,0:T(8,128)(2,1)S(1)}, bf16[208,128]{1,0:T(8,128)(2,1)S(1)}, u32[]{:S(2)}, u32[]{:S(2)}) collective-permute-start(bf16[208,128]{1,0:T(8,128)(2,1)S(1)} %get-tuple-element.34), channel_id=1, source_target_pairs={{0,1},{1,0},{2,3},{3,2},{4,5},{5,4},{6,7},{7,6},{8,9},{9,8},{10,11... | collective-permute-start | bytes 159752 | tf_op jit(solution)/shard_map/ppermute | solution.py:67
  31.7 1.5 %collective-permute-done.10 = bf16[208,128]{1,0:T(8,128)(2,1)S(1)} collective-permute-done((bf16[208,128]{1,0:T(8,128)(2,1)S(1)}, bf16[208,128]{1,0:T(8,128)(2,1)S(1)}, u32[]{:S(2)}, u32[]{:S(2)}) %collective-permute-start.10) | collective-permute-done | bytes 53280 | tf_op jit(solution)/shard_map/ppermute | solution.py:67
  33.2 1.1 %collective-permute-done.11 = bf16[208,128]{1,0:T(8,128)(2,1)S(1)} collective-permute-done((bf16[208,128]{1,0:T(8,128)(2,1)S(1)}, bf16[208,128]{1,0:T(8,128)(2,1)S(1)}, u32[]{:S(2)}, u32[]{:S(2)}) %collective-permute-start.11) | collective-permute-done | bytes 53280 | tf_op jit(solution)/shard_map/ppermute | solution.py:67
  34.4 1.6 %collective-permute-start.15 = (bf16[832,128]{1,0:T(8,128)(2,1)S(1)}, bf16[832,128]{1,0:T(8,128)(2,1)S(1)}, u32[]{:S(2)}, u32[]{:S(2)}) collective-permute-start(bf16[832,128]{1,0:T(8,128)(2,1)S(1)} %pad_maximum_fusion.refs_3_), channel_id=1, source_target_pairs={{0,16},{1,17},{2,18},{3,19},{4,12},{5,13},{6,14},{7,15},{8,24},{9,... | collective-permute-start | bytes 638984 | tf_op jit(solution)/shard_map/ppermute | solution.py:67
  36.0 1.4 %collective-permute-start.16 = (bf16[832,128]{1,0:T(8,128)(2,1)S(1)}, bf16[832,128]{1,0:T(8,128)(2,1)S(1)}, u32[]{:S(2)}, u32[]{:S(2)}) collective-permute-start(bf16[832,128]{1,0:T(8,128)(2,1)S(1)} %pad_maximum_fusion.refs_3_), channel_id=1, source_target_pairs={{0,8},{1,9},{2,10},{3,11},{4,20},{5,21},{6,22},{7,23},{8,0},{9,1},... | collective-permute-start | bytes 638984 | tf_op jit(solution)/shard_map/ppermute | solution.py:67
  38.1 2.5 %collective-permute-done.15.refs_0_ = bf16[832,128]{1,0:T(8,128)(2,1)S(1)} collective-permute-done((bf16[832,128]{1,0:T(8,128)(2,1)S(1)}, bf16[832,128]{1,0:T(8,128)(2,1)S(1)}, u32[]{:S(2)}, u32[]{:S(2)}) %collective-permute-start.15) | collective-permute-done | bytes 213024 | tf_op jit(solution)/shard_map/ppermute | solution.py:67
  40.6 1.2 %collective-permute-done.16.refs_1_ = bf16[832,128]{1,0:T(8,128)(2,1)S(1)} collective-permute-done((bf16[832,128]{1,0:T(8,128)(2,1)S(1)}, bf16[832,128]{1,0:T(8,128)(2,1)S(1)}, u32[]{:S(2)}, u32[]{:S(2)}) %collective-permute-start.16) | collective-permute-done | bytes 213024 | tf_op jit(solution)/shard_map/ppermute | solution.py:67
  41.8 2.3 %collective-permute-done.13.refs_2_ = bf16[832,128]{1,0:T(8,128)(2,1)S(1)} collective-permute-done((bf16[832,128]{1,0:T(8,128)(2,1)S(1)}, bf16[832,128]{1,0:T(8,128)(2,1)S(1)}, u32[]{:S(2)}, u32[]{:S(2)}) %collective-permute-start.13) | collective-permute-done | bytes 213024 | tf_op jit(solution)/shard_map/ppermute | solution.py:67
  44.2 0.7 %multiply_subtract_fusion = (f32[26624]{0:T(1024)}, f32[26624]{0:T(1024)}, f32[26624]{0:T(1024)}) fusion(f32[26624]{0:T(1024)S(1)} %copy-done.1, f32[]{:T(128)} %bitcast.3, f32[]{:T(128)} %bitcast.2, f32[]{:T(128)} %bitcast.12, f32[26624]{0:T(1024)S(1)} %get-tuple-element.31, f32[26624]{0:T(1024)S(1)} %copy-done.2, f32[26624]{0:T(1024)S(1)} %copy-done.3), kind=kLoop, calls=%fused_computation.23 | loop fusion | flops 346112 | bytes 745484 | tf_op jit(solution)/shard_map/sub | solution.py:26
  44.9 1.4 %shard_map.97.refs_1_ = bf16[6656,128]{1,0:T(8,128)(2,1)} custom-call(bf16[832,128]{1,0:T(8,128)(2,1)S(1)} %collective-permute-done.15.refs_0_, bf16[832,128]{1,0:T(8,128)(2,1)S(1)} %collective-permute-done.16.refs_1_, bf16[832,128]{1,0:T(8,128)(2,1)S(1)} %collective-permute-done.13.refs_2_, bf16[832,128]{1,0:T(8,128)(2,1)S(1)} %pad_maximum_fusion.refs_3_, ...), custom_call_target="tpu_custom_call" | custom-call | flops 851968 | bytes 3407872 | tf_op jit(solution)/shard_map/pallas_call | solution.py:154
  46.3 0.7 %shard_map.98 = bf16[6656,128]{1,0:T(8,128)(2,1)} custom-call(bf16[832,128]{1,0:T(8,128)(2,1)S(1)} %collective-permute-done.14.refs_0_, bf16[6656,128]{1,0:T(8,128)(2,1)} %shard_map.97.refs_1_), custom_call_target="tpu_custom_call", output_to_operand_aliasing={{}: (1, {})} | custom-call | flops 851968 | bytes 3407872 | tf_op jit(solution)/shard_map/pallas_call | solution.py:154
  (45 shorter events, 2.9 us)
Async XLA Ops:
  0.6 2.2 %copy-start = (bf16[1,851968]{1,0:T(2,128)(2,1)S(1)}, bf16[1,851968]{1,0:T(2,128)(2,1)}, u32[]{:S(2)}) copy-start(bf16[1,851968]{1,0:T(2,128)(2,1)} %g_ref.7) | copy-start | bytes 5111812
  1.9 1.8 %collective-permute-start.3 = (bf16[832,128]{1,0:T(8,128)(2,1)S(1)}, bf16[832,128]{1,0:T(8,128)(2,1)S(1)}, u32[]{:S(2)}, u32[]{:S(2)}) collective-permute-start(bf16[832,128]{1,0:T(8,128)(2,1)S(1)} %shard_map.93.refs_0_), channel_id=1, source_target_pairs={{0,4},{4,0},{8,12},{12,8},{1,5},{5,1},{9,13},{13,9},{2,6},{6,2},{1... | collective-permute-start | bytes 638984 | tf_op jit(solution)/shard_map/ppermute | solution.py:70
  2.9 3.9 %collective-permute-start.1 = (bf16[832,128]{1,0:T(8,128)(2,1)S(1)}, bf16[832,128]{1,0:T(8,128)(2,1)S(1)}, u32[]{:S(2)}, u32[]{:S(2)}) collective-permute-start(bf16[832,128]{1,0:T(8,128)(2,1)S(1)} %get-tuple-element.19.refs_0_), channel_id=1, source_target_pairs={{0,4},{4,0},{8,12},{12,8},{1,5},{5,1},{9,13},{13,9},{2,6},{6,2},{1... | collective-permute-start | bytes 638984 | tf_op jit(solution)/shard_map/ppermute | solution.py:70
  3.5 4.0 %collective-permute-start = (bf16[1664,128]{1,0:T(8,128)(2,1)S(1)}, bf16[1664,128]{1,0:T(8,128)(2,1)S(1)}, u32[]{:S(2)}, u32[]{:S(2)}) collective-permute-start(bf16[1664,128]{1,0:T(8,128)(2,1)S(1)} %get-tuple-element.21), channel_id=1, source_target_pairs={{0,4},{4,0},{8,12},{12,8},{1,5},{5,1},{9,13},{13,9},{2,6},{6,2},{1... | collective-permute-start | bytes 1277960 | tf_op jit(solution)/shard_map/ppermute | solution.py:70
  3.8 6.9 %collective-permute-start.4 = (bf16[832,128]{1,0:T(8,128)(2,1)S(1)}, bf16[832,128]{1,0:T(8,128)(2,1)S(1)}, u32[]{:S(2)}, u32[]{:S(2)}) collective-permute-start(bf16[832,128]{1,0:T(8,128)(2,1)S(1)} %add_convert_fusion.1), channel_id=1, source_target_pairs={{0,16},{1,17},{2,18},{3,19},{4,12},{5,13},{6,14},{7,15},{8,24},{9,... | collective-permute-start | bytes 638984 | tf_op jit(solution)/shard_map/ppermute | solution.py:67
  6.9 6.1 %collective-permute-start.2 = (bf16[832,128]{1,0:T(8,128)(2,1)S(1)}, bf16[832,128]{1,0:T(8,128)(2,1)S(1)}, u32[]{:S(2)}, u32[]{:S(2)}) collective-permute-start(bf16[832,128]{1,0:T(8,128)(2,1)S(1)} %add_convert_fusion.2), channel_id=1, source_target_pairs={{0,16},{1,17},{2,18},{3,19},{4,12},{5,13},{6,14},{7,15},{8,24},{9,... | collective-permute-start | bytes 638984 | tf_op jit(solution)/shard_map/ppermute | solution.py:67
  10.8 4.8 %collective-permute-start.5 = (bf16[416,128]{1,0:T(8,128)(2,1)S(1)}, bf16[416,128]{1,0:T(8,128)(2,1)S(1)}, u32[]{:S(2)}, u32[]{:S(2)}) collective-permute-start(bf16[416,128]{1,0:T(8,128)(2,1)S(1)} %get-tuple-element.42), channel_id=1, source_target_pairs={{0,8},{1,9},{2,10},{3,11},{4,20},{5,21},{6,22},{7,23},{8,0},{9,1},... | collective-permute-start | bytes 319496 | tf_op jit(solution)/shard_map/ppermute | solution.py:67
  12.8 4.7 %collective-permute-start.6 = (bf16[416,128]{1,0:T(8,128)(2,1)S(1)}, bf16[416,128]{1,0:T(8,128)(2,1)S(1)}, u32[]{:S(2)}, u32[]{:S(2)}) collective-permute-start(bf16[416,128]{1,0:T(8,128)(2,1)S(1)} %get-tuple-element.41), channel_id=1, source_target_pairs={{0,8},{1,9},{2,10},{3,11},{4,20},{5,21},{6,22},{7,23},{8,0},{9,1},... | collective-permute-start | bytes 319496 | tf_op jit(solution)/shard_map/ppermute | solution.py:67
  12.9 15.0 %copy-start.1 = (f32[26624]{0:T(1024)S(1)}, f32[26624]{0:T(1024)}, u32[]{:S(2)}) copy-start(f32[26624]{0:T(1024)} %param.7) | copy-start | bytes 319492
  13.0 15.0 %copy-start.2 = (f32[26624]{0:T(1024)S(1)}, f32[26624]{0:T(1024)}, u32[]{:S(2)}) copy-start(f32[26624]{0:T(1024)} %param.9) | copy-start | bytes 319492
  13.0 15.0 %copy-start.3 = (f32[26624]{0:T(1024)S(1)}, f32[26624]{0:T(1024)}, u32[]{:S(2)}) copy-start(f32[26624]{0:T(1024)} %param.8) | copy-start | bytes 319492
  17.6 5.8 %collective-permute-start.9 = (bf16[208,128]{1,0:T(8,128)(2,1)S(1)}, bf16[208,128]{1,0:T(8,128)(2,1)S(1)}, u32[]{:S(2)}, u32[]{:S(2)}) collective-permute-start(bf16[208,128]{1,0:T(8,128)(2,1)S(1)} %slice.78), channel_id=1, source_target_pairs={{0,1},{1,0},{2,3},{3,2},{4,5},{5,4},{6,7},{7,6},{8,9},{9,8},{10,11... | collective-permute-start | bytes 159752 | tf_op jit(solution)/shard_map/ppermute | solution.py:67
  19.2 6.2 %collective-permute-start.7 = (bf16[208,128]{1,0:T(8,128)(2,1)S(1)}, bf16[208,128]{1,0:T(8,128)(2,1)S(1)}, u32[]{:S(2)}, u32[]{:S(2)}) collective-permute-start(bf16[208,128]{1,0:T(8,128)(2,1)S(1)} %get-tuple-element.44), channel_id=1, source_target_pairs={{0,2},{1,3},{2,0},{3,1},{4,6},{5,7},{6,4},{7,5},{8,10},{9,11},{10,... | collective-permute-start | bytes 159752 | tf_op jit(solution)/shard_map/ppermute | solution.py:67
  21.8 6.2 %collective-permute-start.8 = (bf16[208,128]{1,0:T(8,128)(2,1)S(1)}, bf16[208,128]{1,0:T(8,128)(2,1)S(1)}, u32[]{:S(2)}, u32[]{:S(2)}) collective-permute-start(bf16[208,128]{1,0:T(8,128)(2,1)S(1)} %get-tuple-element.43), channel_id=1, source_target_pairs={{0,3},{1,2},{2,1},{3,0},{4,7},{5,6},{6,5},{7,4},{8,11},{9,10},{10,... | collective-permute-start | bytes 159752 | tf_op jit(solution)/shard_map/ppermute | solution.py:67
  28.1 5.1 %collective-permute-start.10 = (bf16[208,128]{1,0:T(8,128)(2,1)S(1)}, bf16[208,128]{1,0:T(8,128)(2,1)S(1)}, u32[]{:S(2)}, u32[]{:S(2)}) collective-permute-start(bf16[208,128]{1,0:T(8,128)(2,1)S(1)} %get-tuple-element.34), channel_id=1, source_target_pairs={{0,2},{1,3},{2,0},{3,1},{4,6},{5,7},{6,4},{7,5},{8,10},{9,11},{10,... | collective-permute-start | bytes 159752 | tf_op jit(solution)/shard_map/ppermute | solution.py:67
  28.2 6.1 %collective-permute-start.11 = (bf16[208,128]{1,0:T(8,128)(2,1)S(1)}, bf16[208,128]{1,0:T(8,128)(2,1)S(1)}, u32[]{:S(2)}, u32[]{:S(2)}) collective-permute-start(bf16[208,128]{1,0:T(8,128)(2,1)S(1)} %get-tuple-element.34), channel_id=1, source_target_pairs={{0,3},{1,2},{2,1},{3,0},{4,7},{5,6},{6,5},{7,4},{8,11},{9,10},{10,... | collective-permute-start | bytes 159752 | tf_op jit(solution)/shard_map/ppermute | solution.py:67
  29.1 5.2 %collective-permute-start.12 = (bf16[208,128]{1,0:T(8,128)(2,1)S(1)}, bf16[208,128]{1,0:T(8,128)(2,1)S(1)}, u32[]{:S(2)}, u32[]{:S(2)}) collective-permute-start(bf16[208,128]{1,0:T(8,128)(2,1)S(1)} %get-tuple-element.34), channel_id=1, source_target_pairs={{0,1},{1,0},{2,3},{3,2},{4,5},{5,4},{6,7},{7,6},{8,9},{9,8},{10,11... | collective-permute-start | bytes 159752 | tf_op jit(solution)/shard_map/ppermute | solution.py:67
  34.4 6.2 %collective-permute-start.15 = (bf16[832,128]{1,0:T(8,128)(2,1)S(1)}, bf16[832,128]{1,0:T(8,128)(2,1)S(1)}, u32[]{:S(2)}, u32[]{:S(2)}) collective-permute-start(bf16[832,128]{1,0:T(8,128)(2,1)S(1)} %pad_maximum_fusion.refs_3_), channel_id=1, source_target_pairs={{0,16},{1,17},{2,18},{3,19},{4,12},{5,13},{6,14},{7,15},{8,24},{9,... | collective-permute-start | bytes 638984 | tf_op jit(solution)/shard_map/ppermute | solution.py:67
  36.0 5.8 %collective-permute-start.16 = (bf16[832,128]{1,0:T(8,128)(2,1)S(1)}, bf16[832,128]{1,0:T(8,128)(2,1)S(1)}, u32[]{:S(2)}, u32[]{:S(2)}) collective-permute-start(bf16[832,128]{1,0:T(8,128)(2,1)S(1)} %pad_maximum_fusion.refs_3_), channel_id=1, source_target_pairs={{0,8},{1,9},{2,10},{3,11},{4,20},{5,21},{6,22},{7,23},{8,0},{9,1},... | collective-permute-start | bytes 638984 | tf_op jit(solution)/shard_map/ppermute | solution.py:67
  37.4 6.7 %collective-permute-start.13 = (bf16[832,128]{1,0:T(8,128)(2,1)S(1)}, bf16[832,128]{1,0:T(8,128)(2,1)S(1)}, u32[]{:S(2)}, u32[]{:S(2)}) collective-permute-start(bf16[832,128]{1,0:T(8,128)(2,1)S(1)} %pad_maximum_fusion.refs_3_), channel_id=1, source_target_pairs={{0,24},{1,25},{2,26},{3,27},{4,28},{5,29},{6,30},{7,31},{8,16},{9,... | collective-permute-start | bytes 638984 | tf_op jit(solution)/shard_map/ppermute | solution.py:67
  38.0 6.9 %collective-permute-start.19 = (bf16[832,128]{1,0:T(8,128)(2,1)S(1)}, bf16[832,128]{1,0:T(8,128)(2,1)S(1)}, u32[]{:S(2)}, u32[]{:S(2)}) collective-permute-start(bf16[832,128]{1,0:T(8,128)(2,1)S(1)} %pad_maximum_fusion.refs_3_), channel_id=1, source_target_pairs={{0,4},{4,0},{8,12},{12,8},{1,5},{5,1},{9,13},{13,9},{2,6},{6,2},{1... | collective-permute-start | bytes 638984 | tf_op jit(solution)/shard_map/ppermute | solution.py:70
  40.6 4.3 %collective-permute-start.17 = (bf16[832,128]{1,0:T(8,128)(2,1)S(1)}, bf16[832,128]{1,0:T(8,128)(2,1)S(1)}, u32[]{:S(2)}, u32[]{:S(2)}) collective-permute-start(bf16[832,128]{1,0:T(8,128)(2,1)S(1)} %collective-permute-done.15.refs_0_), channel_id=1, source_target_pairs={{0,4},{4,0},{8,12},{12,8},{1,5},{5,1},{9,13},{13,9},{2,6},{6,2},{1... | collective-permute-start | bytes 638984 | tf_op jit(solution)/shard_map/ppermute | solution.py:70
  41.8 3.1 %collective-permute-start.18 = (bf16[832,128]{1,0:T(8,128)(2,1)S(1)}, bf16[832,128]{1,0:T(8,128)(2,1)S(1)}, u32[]{:S(2)}, u32[]{:S(2)}) collective-permute-start(bf16[832,128]{1,0:T(8,128)(2,1)S(1)} %collective-permute-done.16.refs_1_), channel_id=1, source_target_pairs={{0,4},{4,0},{8,12},{12,8},{1,5},{5,1},{9,13},{13,9},{2,6},{6,2},{1... | collective-permute-start | bytes 638984 | tf_op jit(solution)/shard_map/ppermute | solution.py:70
  44.2 2.1 %collective-permute-start.14 = (bf16[832,128]{1,0:T(8,128)(2,1)S(1)}, bf16[832,128]{1,0:T(8,128)(2,1)S(1)}, u32[]{:S(2)}, u32[]{:S(2)}) collective-permute-start(bf16[832,128]{1,0:T(8,128)(2,1)S(1)} %collective-permute-done.13.refs_2_), channel_id=1, source_target_pairs={{0,4},{4,0},{8,12},{12,8},{1,5},{5,1},{9,13},{13,9},{2,6},{6,2},{1... | collective-permute-start | bytes 638984 | tf_op jit(solution)/shard_map/ppermute | solution.py:70
